TPU v7x, 512 devices: a whole 4x8x8 slice. The times are simulated.
512 devices in a mesh: ep: 128 (over y, z, core), dp: 4 (over x).
Axes of the slice: x: 4, y: 8, z: 8, core: 2. Of those that a mesh axis runs over, the one named last changes fastest.
Arguments:
- tokens: bfloat16 [8192, 3584], P(('ep', 'dp')), may hold values from -6 to 6
- norm_gain: float32 [3584], replicated, may hold values from 0.25 to 1.75
- router: bfloat16 [3584, 128], replicated, may hold values from -0.09375 to 0.09375
- next_router: bfloat16 [3584, 128], P('dp'), may hold values from -0.09375 to 0.09375
- expert_ids: int32 [8192, 8], P(('ep', 'dp')), may hold values from 0 to 127, all different within a row; in each aligned block of 16 rows (0 to 15, 16 to 31, ...) at most 2 rows name the same one
- store: bfloat16 [128, 4, 112, 128, 128], P('ep', 'dp'), may hold values from -0.125 to 0.125
- send_list: int32 [128, 128], P('ep'), may hold values from -1 to 111, as said below
- cache_map: int32 [128, 112], P('ep'), may hold values from 0 to 127, as said below
Outputs:
- layer_out: bfloat16 [8192, 3584], P(('ep', 'dp'))
- next_scores: float32 [8192, 128], P(('ep', 'dp'))
Inputs may be any that keep to these rules, and one draw needn't show every extreme that they name: `expert_ids`: each row names 8 different experts; among the rows of one device no expert is named by more than 2 rows, a bound that some block reaches. `send_list`: an entry is -1 where that arriving slot stays empty; every row names each of the 112 store indices exactly once. `cache_map`: each entry numbers an arriving slot of that device that is never empty; the entries of a row are distinct.
All inputs are finite; a program needn't handle non-finite values.
Results may differ from a plain program's by a relative error of at most 0.0095.
Values may be sent and summed in bfloat16 or wider, within the bound.
A program may use at most 64 MiB of HBM per device.

v0:
```python
import jax
import jax.numpy as jnp
from jax import lax
from jax.sharding import PartitionSpec as P


def cut_along(x, dim, devices):
    before, after = (x.shape[:dim], x.shape[dim + 1 :])
    return jnp.moveaxis(x.reshape(*before, devices, -1, *after), dim, 0)


def laid_out(parts, dim):
    lengths = list(parts.shape[1:])
    lengths[dim] *= parts.shape[0]
    return jnp.moveaxis(parts, 0, dim).reshape(lengths)


def exchange_both(x, axis, axes, splits, concats):
    sizes = [lax.axis_size(a) for a in axes]
    parts = cut_along(x, splits[0], sizes[0])
    parts = jnp.moveaxis(cut_along(parts, splits[1] + 1, sizes[1]), 0, 1)
    inside = parts.shape[2:]
    parts = parts.reshape(-1, *inside)
    parts = lax.all_to_all(parts, axis, split_axis=0, concat_axis=0, tiled=True)
    parts = laid_out(parts.reshape(*sizes, *inside), concats[0] + 1)
    return laid_out(parts, concats[1])


def summed_on_arrival(x, axis, dim):
    devices = lax.axis_size(axis)
    parts = lax.all_to_all(cut_along(x, dim, devices), axis, 0, 0, tiled=True)
    return jnp.sum(parts.astype(jnp.float32), axis=0)


def from_everyone(x, axis):
    devices = lax.axis_size(axis)
    return lax.all_to_all(jnp.broadcast_to(x[None], (devices, *x.shape)), axis, 0, 0, tiled=True)


def gathered_copies(x, axis, dim):
    parts = from_everyone(x, axis)
    return laid_out(parts, dim)


def per_device(tokens, norm_gain, router, next_router, expert_ids, store, send_list, cache_map):
    tok_dev, width = tokens.shape
    n_dp = lax.axis_size("dp")
    experts = router.shape[1]
    top = expert_ids.shape[1]
    tiles = cache_map.shape[1]
    tile_rows = store.shape[3]
    tile_cols = store.shape[4]
    part = width // n_dp
    row_tiles = part // tile_rows
    col_tiles = tiles // (2 * row_tiles)
    hidden_width = col_tiles * tile_cols
    capacity = min(tok_dev, max(2, 2 * tok_dev * top // experts))
    values = tokens.astype(jnp.float32)
    scale = lax.rsqrt(jnp.mean(values * values, axis=1, keepdims=True) + 1e-06)
    normed = (values * scale * norm_gain).astype(jnp.bfloat16)
    scores = jax.nn.sigmoid(jnp.dot(normed, router, preferred_element_type=jnp.float32))
    chosen = (expert_ids[:, :, None] == jnp.arange(experts, dtype=jnp.int32)[None, None, :]).astype(
        jnp.float32
    )
    picked = jnp.sum(chosen * scores[:, None, :], axis=2)
    weights = (2.5 * picked / jnp.sum(picked, axis=1, keepdims=True)).astype(jnp.bfloat16)
    flat = chosen.reshape(tok_dev * top, experts)
    before = jnp.cumsum(flat, axis=0) - flat
    rank = jnp.sum(before * flat, axis=1).astype(jnp.int32)
    slot = expert_ids.reshape(-1) * capacity + rank
    columns = jnp.arange(experts * capacity, dtype=jnp.int32)
    match = (slot[:, None] == columns[None, :]).reshape(tok_dev, top, experts * capacity)
    dispatch = jnp.sum(match.astype(jnp.float32), axis=1).astype(jnp.bfloat16)
    combine = jnp.sum(
        jnp.where(match, weights.astype(jnp.float32)[:, :, None], 0.0), axis=1
    ).astype(jnp.bfloat16)
    outgoing = lax.dot_general(
        dispatch, normed, (((0,), (0,)), ((), ())), preferred_element_type=jnp.float32
    ).astype(jnp.bfloat16)
    owned = store.reshape(tiles, tile_rows, tile_cols)
    wanted = send_list.reshape(-1)
    present = wanted >= 0
    leaving = jnp.where(
        present[:, None, None], owned[jnp.maximum(wanted, 0)], jnp.zeros((), jnp.bfloat16)
    )
    arrived = lax.all_to_all(leaving, "ep", split_axis=0, concat_axis=0, tiled=True)
    cached = arrived[cache_map.reshape(-1)].reshape(2, row_tiles, col_tiles, tile_rows, tile_cols)
    up_tiles = cached[0]
    down_tiles = cached[1]
    rows = exchange_both(outgoing, ("dp", "ep"), ("dp", "ep"), (1, 0), (1, 0)).reshape(-1, part)
    count = rows.shape[0]

    def down_rows(hidden):
        number = hidden.shape[0]
        product = jnp.einsum(
            "ncs,acts->nat",
            hidden.reshape(number, col_tiles, tile_cols),
            down_tiles,
            preferred_element_type=jnp.float32,
        )
        return product.reshape(number, part).astype(jnp.bfloat16)

    block = rows.reshape(count // n_dp * lax.axis_size("dp"), row_tiles, tile_rows)
    product = jnp.einsum("nat,acts->ncs", block, up_tiles, preferred_element_type=jnp.float32)
    share = summed_on_arrival(
        product.reshape(count // n_dp * lax.axis_size("dp"), hidden_width).astype(jnp.bfloat16),
        "dp",
        0,
    )
    activated = jax.nn.silu(share).astype(jnp.bfloat16)
    result = (lambda piece, start: down_rows(piece))(
        gathered_copies(activated, "dp", 0), jnp.int32(0)
    )
    back = exchange_both(
        result.reshape(-1, n_dp * part), ("ep", "dp"), ("ep", "dp"), (0, 1), (0, 1)
    )
    mixed = jnp.dot(combine, back, preferred_element_type=jnp.float32)
    layer_out = (values + mixed).astype(jnp.bfloat16)
    stream = layer_out.astype(jnp.float32)
    renorm = lax.rsqrt(jnp.mean(stream * stream, axis=1, keepdims=True) + 1e-06)
    next_normed = (stream * renorm).astype(jnp.bfloat16)
    features = lax.all_to_all(next_normed, "dp", split_axis=1, concat_axis=0, tiled=True)
    partial_scores = jnp.dot(features, next_router, preferred_element_type=jnp.float32)
    next_logits = summed_on_arrival(partial_scores.astype(jnp.bfloat16), "dp", 0)
    return (layer_out, jax.nn.sigmoid(next_logits))


def solution(mesh):
    in_specs = (
        P(("ep", "dp"), None),
        P(),
        P(),
        P("dp", None),
        P(("ep", "dp"), None),
        P("ep", "dp", None, None, None),
        P("ep", None),
        P("ep", None),
    )
    out_specs = (P(("ep", "dp"), None), P(("ep", "dp"), None))
    return jax.shard_map(
        per_device, mesh=mesh, in_specs=in_specs, out_specs=out_specs, check_vma=False
    )
```

profile of v0, /device:TPU:8, one launch (start us, length us, event | category | flops | bytes accessed | tf_op | source)
XLA Modules:
  0.0 357.7 jit_solution(262822518069316782)
XLA Ops:
  0.6 0.0 copy-start
  0.6 1.1 fusion.11
  1.8 0.8 copy.28
  2.5 0.1 eq.36
  2.6 0.0 copy-done
  2.6 1.2 fusion.8
  3.8 0.3 select_reduce_fusion.1
  4.1 0.1 fusion.14
  4.2 0.2 reduce_window_sum.11
  4.4 0.2 select_reduce_fusion.3
  4.6 0.1 convert_element_type.80
  4.7 0.1 fusion.19
  4.8 0.2 select_reduce_fusion
  4.9 1.6 convolution_convert_fusion
  6.5 0.1 copy.53
  6.7 1.7 reshape_reshape.6
  8.4 0.0 copy-start.5
  8.4 21.1 %all-to-all-start = ((bf16[512,2,896]{2,1,0:T(2,128)(2,1)}), bf16[512,2,896]{2,1,0:T(2,128)(2,1)S(1)}, u32[]{:S(2)}, u32[]{:S(2)}) async-start(bf16[512,2,896]{2,1,0:T(2,128)(2,1)} %reshape_reshape.6), calls=%async_computation | async-start | bytes 3670016 | tf_op jit(solution)/shard_map/all_to_all | solution.py:24
  29.5 0.0 copy-done.5
  29.5 5.1 %gather_fusion = bf16[128,128,128]{2,1,0:T(8,128)(2,1)} fusion(bf16[112,128,128]{2,1,0:T(8,128)(2,1)} %bitcast.73, s32[1024]{0:T(1024)S(1)} %pad_clamp_fusion.1), kind=kCustom, calls=%fused_computation | custom fusion | bytes 8389120 | tf_op jit(solution)/shard_map/gather | solution.py:84
  34.6 4.5 %broadcast_select_fusion = bf16[128,128,128]{2,1,0:T(8,128)(2,1)} fusion(bf16[128,128,128]{2,1,0:T(8,128)(2,1)} %gather_fusion, pred[128]{0:T(512)(128)(4,1)S(1)} %compare_bitcast_fusion), kind=kLoop, calls=%fused_computation.7 | loop fusion | flops 2097152 | bytes 8388736 | tf_op jit(solution)/shard_map/jit(_where)/select_n | solution.py:83
  39.1 0.0 copy-start.6
  39.2 38.5 %all-to-all-done = bf16[512,2,896]{2,1,0:T(2,128)(2,1)S(1)} async-done(((bf16[512,2,896]{2,1,0:T(2,128)(2,1)}), bf16[512,2,896]{2,1,0:T(2,128)(2,1)S(1)}, u32[]{:S(2)}, u32[]{:S(2)}) %all-to-all-start) | async-done | bytes 1835040 | tf_op jit(solution)/shard_map/all_to_all | solution.py:24
  77.7 8.6 %all-to-all-start.1 = ((bf16[128,128,128]{2,1,0:T(8,128)(2,1)}), bf16[128,128,128]{2,1,0:T(8,128)(2,1)}, u32[]{:S(2)}, u32[]{:S(2)}) async-start(bf16[128,128,128]{2,1,0:T(8,128)(2,1)} %broadcast_select_fusion), calls=%async_computation.1 | async-start | bytes 8388608 | tf_op jit(solution)/shard_map/all_to_all | solution.py:86
  86.3 0.0 copy-done.6
  86.3 3.6 %copy.54 = bf16[4,128,2,896]{3,0,2,1:T(4,128)(2,1)} copy(bf16[4,128,2,896]{3,2,1,0:T(2,128)(2,1)S(1)} %bitcast.65) | data formatting | bytes 3670016 | tf_op jit(solution)/shard_map/reshape | solution.py:25
  89.9 4.3 %reshape_reshape_reshape_reshape.3 = bf16[1024,7,128]{2,1,0:T(8,128)(2,1)} reshape(bf16[128,2,4,896]{3,2,1,0:T(4,128)(2,1)} %bitcast.72) | data formatting | bytes 3670016 | tf_op jit(solution)/shard_map/reshape;reshape;reshape;reshape | solution.py:103
  94.2 88.3 %all-to-all-done.1 = bf16[128,128,128]{2,1,0:T(8,128)(2,1)} async-done(((bf16[128,128,128]{2,1,0:T(8,128)(2,1)}), bf16[128,128,128]{2,1,0:T(8,128)(2,1)}, u32[]{:S(2)}, u32[]{:S(2)}) %all-to-all-start.1) | async-done | bytes 4194336 | tf_op jit(solution)/shard_map/all_to_all | solution.py:86
  182.5 5.1 %gather_fusion.1 = bf16[112,128,128]{2,1,0:T(8,128)(2,1)} fusion(bf16[128,128,128]{2,1,0:T(8,128)(2,1)} %all-to-all-done.1, s32[1024]{0:T(1024)S(1)} %pad_clamp_fusion), kind=kCustom, calls=%fused_computation.1 | custom fusion | bytes 7340480 | tf_op jit(solution)/shard_map/gather | solution.py:87
  187.5 3.7 %fusion.21 = (bf16[56,128,128]{2,1,0:T(8,128)(2,1)S(1)}, bf16[56,128,128]{2,1,0:T(8,128)(2,1)}) fusion(bf16[112,128,128]{2,1,0:T(8,128)(2,1)} %gather_fusion.1), kind=kLoop, calls=%fused_computation.54 | loop fusion | bytes 7340032 | tf_op jit(solution)/shard_map/slice | solution.py:88
  191.2 2.5 copy.33
  193.8 4.5 %bitcast_convert_fusion = bf16[1024,1024]{1,0:T(8,128)(2,1)S(1)} fusion(bf16[1024,7,128]{2,0,1:T(8,128)(2,1)} %bitcast.77, bf16[1024,7,128]{2,1,0:T(8,128)(2,1)} %reshape_reshape_reshape_reshape.3), kind=kOutput, calls=%fused_computation.5 | convolution fusion | flops 1880096768 | bytes 5767168 | tf_op jit(solution)/shard_map/nat,acts->ncs/dot_general | solution.py:104
  198.3 28.5 %all_to_all.49 = bf16[4,256,1024]{2,1,0:T(8,128)(2,1)S(1)} all-to-all(bf16[4,256,1024]{2,1,0:T(8,128)(2,1)S(1)} %bitcast.74), channel_id=1, replica_groups=mesh['ep'=128,'dp'=4] {'dp'}, dimensions={0} | all-to-all | bytes 4194304 | tf_op jit(solution)/shard_map/all_to_all | solution.py:31
  226.8 0.4 convert_reduce_fusion
  227.2 0.3 multiply_convert_fusion
  227.5 1.6 broadcast_in_dim.30
  229.1 3.6 %all-to-all-start.3 = ((bf16[4,256,1024]{2,1,0:T(8,128)(2,1)}), bf16[4,256,1024]{2,1,0:T(8,128)(2,1)S(1)}, u32[]{:S(2)}, u32[]{:S(2)}) async-start(bf16[4,256,1024]{2,1,0:T(8,128)(2,1)} %broadcast_in_dim.30), calls=%async_computation.3 | async-start | bytes 4194304 | tf_op jit(solution)/shard_map/all_to_all | solution.py:37
  232.7 3.0 copy.35
  235.7 21.8 %all-to-all-done.3 = bf16[4,256,1024]{2,1,0:T(8,128)(2,1)S(1)} async-done(((bf16[4,256,1024]{2,1,0:T(8,128)(2,1)}), bf16[4,256,1024]{2,1,0:T(8,128)(2,1)S(1)}, u32[]{:S(2)}, u32[]{:S(2)}) %all-to-all-start.3) | async-done | bytes 2097184 | tf_op jit(solution)/shard_map/all_to_all | solution.py:37
  257.5 0.0 copy-start.1
  257.5 0.6 copy.43
  258.1 0.9 copy-done.1
  259.0 3.6 %bitcast_convert_fusion.1 = bf16[1024,896]{1,0:T(8,128)(2,1)} fusion(bf16[896,8,128]{2,0,1:T(8,128)(2,1)S(1)} %bitcast.76, bf16[1024,8,128]{2,1,0:T(8,128)(2,1)S(1)} %bitcast.75), kind=kOutput, calls=%fused_computation.8 | convolution fusion | flops 1879965696 | bytes 5767168 | tf_op jit(solution)/shard_map/ncs,acts->nat/dot_general | solution.py:95
  262.6 3.1 reshape_reshape_reshape.3
  265.8 1.4 copy.37
  267.2 66.4 %all_to_all.50 = bf16[512,2,896]{2,1,0:T(2,128)(2,1)S(1)} all-to-all(bf16[512,2,896]{2,1,0:T(2,128)(2,1)S(1)} %bitcast.68), channel_id=1, replica_groups=mesh['ep'=128,'dp'=4] {'ep','dp'}, dimensions={0} | all-to-all | bytes 3670016 | tf_op jit(solution)/shard_map/all_to_all | solution.py:24
  333.6 2.0 copy.38
  335.6 0.0 copy-start.2
  335.6 3.1 copy.39
  338.7 0.0 copy-start.4
  338.7 0.0 copy-done.2
  338.7 0.7 fusion.9
  339.4 0.0 copy-start.3
  339.5 0.1 fusion.10
  339.6 9.6 %all_to_all.51 = bf16[16,4,896]{2,0,1:T(8,128)(2,1)S(1)} all-to-all(bf16[16,4,896]{2,0,1:T(8,128)(2,1)S(1)} %bitcast.79), channel_id=1, replica_groups=mesh['ep'=128,'dp'=4] {'dp'}, dimensions={1} | all-to-all | bytes 229376 | tf_op jit(solution)/shard_map/all_to_all | solution.py:122
  349.1 0.0 copy-done.4
  349.2 0.2 convolution_convert_fusion.1
  349.3 7.7 %all_to_all.52 = bf16[4,16,128]{2,1,0:T(8,128)(2,1)S(1)} all-to-all(bf16[4,16,128]{2,1,0:T(8,128)(2,1)S(1)} %bitcast.81), channel_id=1, replica_groups=mesh['ep'=128,'dp'=4] {'dp'}, dimensions={0} | all-to-all | bytes 32768 | tf_op jit(solution)/shard_map/all_to_all | solution.py:31
  357.1 0.6 add_divide_fusion
  357.7 0.0 copy-done.3
  (11 shorter events, 0.1 us)
Async XLA Ops:
  0.6 2.0 copy-start
  8.4 21.1 %copy-start.5 = (s32[1,128]{1,0:T(1,128)S(1)}, s32[1,128]{1,0:T(1,128)}, u32[]{:S(2)}) copy-start(s32[1,128]{1,0:T(1,128)} %param.14) | copy-start | bytes 1540
  8.4 69.3 %all-to-all-start = ((bf16[512,2,896]{2,1,0:T(2,128)(2,1)}), bf16[512,2,896]{2,1,0:T(2,128)(2,1)S(1)}, u32[]{:S(2)}, u32[]{:S(2)}) async-start(bf16[512,2,896]{2,1,0:T(2,128)(2,1)} %reshape_reshape.6), calls=%async_computation | async-start | bytes 3670016 | tf_op jit(solution)/shard_map/all_to_all | solution.py:24
  39.1 47.1 %copy-start.6 = (s32[1,112]{1,0:T(1,128)S(1)}, s32[1,112]{1,0:T(1,128)}, u32[]{:S(2)}) copy-start(s32[1,112]{1,0:T(1,128)} %param.15) | copy-start | bytes 1348
  77.7 104.8 %all-to-all-start.1 = ((bf16[128,128,128]{2,1,0:T(8,128)(2,1)}), bf16[128,128,128]{2,1,0:T(8,128)(2,1)}, u32[]{:S(2)}, u32[]{:S(2)}) async-start(bf16[128,128,128]{2,1,0:T(8,128)(2,1)} %broadcast_select_fusion), calls=%async_computation.1 | async-start | bytes 8388608 | tf_op jit(solution)/shard_map/all_to_all | solution.py:86
  229.1 28.4 %all-to-all-start.3 = ((bf16[4,256,1024]{2,1,0:T(8,128)(2,1)}), bf16[4,256,1024]{2,1,0:T(8,128)(2,1)S(1)}, u32[]{:S(2)}, u32[]{:S(2)}) async-start(bf16[4,256,1024]{2,1,0:T(8,128)(2,1)} %broadcast_in_dim.30), calls=%async_computation.3 | async-start | bytes 4194304 | tf_op jit(solution)/shard_map/all_to_all | solution.py:37
  257.5 1.5 copy-start.1
  335.6 3.1 copy-start.2
  338.7 10.4 %copy-start.4 = (bf16[896,128]{1,0:T(8,128)(2,1)S(1)}, bf16[896,128]{1,0:T(8,128)(2,1)}, u32[]{:S(2)}) copy-start(bf16[896,128]{1,0:T(8,128)(2,1)} %param.11) | copy-start | bytes 688132
  339.4 18.2 %copy-start.3 = (bf16[16,3584]{1,0:T(8,128)(2,1)}, bf16[16,3584]{1,0:T(8,128)(2,1)S(1)}, u32[]{:S(2)}) copy-start(bf16[16,3584]{1,0:T(8,128)(2,1)S(1)} %get-tuple-element.9) | copy-start | bytes 344068
where the time goes:
time: 359 us; the launch traced here: 358 us
  waiting for transfers between devices  149 us (42%)
  blocking collectives  112 us (31%)
  local copies, waits for them, and re-layouts  42.8 us (12%)
  starting transfers between devices  33.3 us (9%)
  matrix products  11.8 us (3%)
  other arithmetic  8.03 us (2%)
    all_to_all x1, waiting for transfers between devices, per_device(): lax.all_to_all(leaving, 'ep', split_axis=0, concat_axis=0, tiled=True)  88.3 us
    all_to_all x1, blocking collectives, exchange_both(): parts = lax.all_to_all(parts, axis, split_axis=0, concat_axis=0, tiled=True)  66.4 us
    all_to_all x1, waiting for transfers between devices, exchange_both(): parts = lax.all_to_all(parts, axis, split_axis=0, concat_axis=0, tiled=True)  38.5 us
    all_to_all x2, blocking collectives, summed_on_arrival(): parts = lax.all_to_all(cut_along(x, dim, devices), axis, 0, 0, tiled=True)  36.2 us
    all_to_all x1, waiting for transfers between devices, from_everyone(): lax.all_to_all(jnp.broadcast_to(x[None], (devices, *x.shape)), axis, 0, 0...  21.8 us
    all_to_all x1, starting transfers between devices, exchange_both(): parts = lax.all_to_all(parts, axis, split_axis=0, concat_axis=0, tiled=True)  21.1 us
    all_to_all x1, blocking collectives, per_device(): lax.all_to_all(next_normed, 'dp', split_axis=1, concat_axis=0, tiled=True)  9.57 us
    all_to_all x1, starting transfers between devices, per_device(): lax.all_to_all(leaving, 'ep', split_axis=0, concat_axis=0, tiled=True)  8.61 us
  transfers between devices with their start and end apart: 3, of which 3 were waited for; matrix products, arithmetic and copies ran while one was open for 6% of the time, Pallas kernels for 0%

commit v1 on v0

v1 whole, which is shorter than its diff:
```python
import functools

import jax
import jax.numpy as jnp
from jax import lax
from jax.experimental import pallas as pl
from jax.experimental.pallas import tpu as pltpu
from jax.sharding import PartitionSpec as P

MESH = pl.DeviceIdType.MESH
CAP = 2
LANES = 128


def place(side):
    e = lax.axis_index("ep")
    x = lax.axis_index("dp")
    y, z, c = e // (2 * side), (e // 2) % side, e % 2
    a = y + c * (z - y)
    b = z + c * (y - z)
    return x, y, z, c, a, b


def on_line(side, a, b, c):
    wide, narrow = 2 * side - c * (2 * side - 2), 2 + c * (2 * side - 2)
    return a * wide + b * narrow


def send(src, dst, send_sem, recv_sem, ep, dp):
    pltpu.make_async_remote_copy(
        src_ref=src,
        dst_ref=dst,
        send_sem=send_sem,
        recv_sem=recv_sem,
        device_id={"ep": ep, "dp": dp},
        device_id_type=MESH,
    ).start()


def wait_bytes(ref, sem):
    pltpu.make_async_copy(ref, ref, sem).wait()


def greet(ep, dp):
    pl.semaphore_signal(
        pltpu.get_barrier_semaphore(), inc=1, device_id={"ep": ep, "dp": dp}, device_id_type=MESH
    )


def each(count, body):
    def step(j, carry):
        body(j)
        return carry

    lax.fori_loop(0, count, step, 0)


def gather_kernel(
    side,
    dps,
    chunks,
    part,
    pay_ref,
    router_ref,
    rows_ref,
    comb_ref,
    routers_ref,
    got,
    send_sem,
    recv_sem,
    router_send,
    router_recv,
):
    x, y, z, c, a, b = place(side)
    line = side * dps
    mine = a * dps + x
    me = lax.axis_index("ep")

    def hello(j):
        k = (mine + 1 + j) % line
        greet(on_line(side, k // dps, b, c) + c, k % dps)

    each(line - 1, hello)
    pl.semaphore_wait(pltpu.get_barrier_semaphore(), line - 1)

    def out(j):
        k = (mine + 1 + j) % line
        send(
            pay_ref.at[k % dps, k // dps],
            got.at[mine],
            send_sem,
            recv_sem,
            on_line(side, k // dps, b, c) + c,
            k % dps,
        )

    each(line - 1, out)

    def router_out(j):
        send(router_ref, routers_ref.at[x], router_send, router_recv, me, (x + 1 + j) % dps)

    each(dps - 1, router_out)
    got[mine] = pay_ref[x, a]
    routers_ref[x] = router_ref[...]
    wait_bytes(got.at[pl.ds(0, line - 1)], recv_sem)

    tok = pay_ref.shape[2]
    blocks = line // chunks
    depth = blocks * tok
    experts = 2 * side
    width = experts * blocks * CAP
    q = lax.broadcasted_iota(jnp.int32, (width, LANES), 0)
    k = lax.broadcasted_iota(jnp.int32, (width, LANES), 1)
    pick_t = (k == (q // (blocks * CAP)) * CAP + q % CAP).astype(jnp.float32).astype(jnp.bfloat16)
    q = lax.broadcasted_iota(jnp.int32, (LANES, width), 1)
    k = lax.broadcasted_iota(jnp.int32, (LANES, width), 0)
    pick = (k == (q // (blocks * CAP)) * CAP + q % CAP).astype(jnp.float32).astype(jnp.bfloat16)
    r = lax.broadcasted_iota(jnp.int32, (depth, width), 0)
    q = lax.broadcasted_iota(jnp.int32, (depth, width), 1)
    own = r // tok == (q % (blocks * CAP)) // CAP
    r = lax.broadcasted_iota(jnp.int32, (width, depth), 1)
    q = lax.broadcasted_iota(jnp.int32, (width, depth), 0)
    own_t = r // tok == (q % (blocks * CAP)) // CAP
    for i in range(chunks):
        piece = got[i * blocks : (i + 1) * blocks].reshape(depth, part + LANES)
        comb = piece[:, part:]
        spread = jnp.dot(comb, pick, preferred_element_type=jnp.float32)
        comb_ref[i] = jnp.where(own, spread, 0.0).astype(jnp.bfloat16)
        spread_t = lax.dot_general(
            pick_t, comb, (((1,), (1,)), ((), ())), preferred_element_type=jnp.float32
        )
        named = jnp.where(own_t & (spread_t != 0.0), 1.0, 0.0).astype(jnp.bfloat16)
        rows = jnp.dot(named, piece[:, :part], preferred_element_type=jnp.float32)
        rows_ref[i] = rows.astype(jnp.bfloat16).reshape(experts, blocks * CAP, part)

    wait_bytes(routers_ref.at[pl.ds(0, dps - 1)], router_recv)
    wait_bytes(routers_ref.at[pl.ds(0, dps - 1)], router_send)
    wait_bytes(got.at[pl.ds(0, line - 1)], send_sem)


def layer_kernel(
    side,
    dps,
    chunks,
    rows_ref,
    comb_ref,
    tiles_hbm,
    map_ref,
    tokens_ref,
    routers_ref,
    out_ref,
    scores_ref,
    tiles,
    up,
    down,
    recv,
    pre,
    sums,
    hid,
    res,
    ret,
    mix,
    fin,
    tile_sem,
    row_send,
    row_recv,
    sum_send,
    sum_recv,
    hid_send,
    hid_recv,
    ret_send,
    ret_recv,
    fin_send,
    fin_recv,
):
    x, y, z, c, a, b = place(side)
    me = lax.axis_index("ep")
    line = side * dps
    mine = a * dps + x
    experts = 2 * side
    as_expert = b * 2 + c
    as_source = c * side + b
    part = up.shape[0]
    hidden = up.shape[1]
    slots = rows_ref.shape[2]
    tok = tokens_ref.shape[0]
    blocks = line // chunks

    tile_copy = pltpu.make_async_copy(tiles_hbm, tiles, tile_sem)
    tile_copy.start()

    def expert_at(d):
        return on_line(side, a, d // 2, c) + d % 2

    def source_at(s):
        other, i = s // side, s % side
        first = y * 2 * side + i * 2
        second = i * 2 * side + z * 2 + 1
        return first + other * (second - first)

    def line_at(k):
        return on_line(side, k // dps, b, c) + c

    def hello_experts(j):
        greet(expert_at((as_expert + 1 + j) % experts), x)

    def hello_sources(j):
        greet(source_at((as_source + 1 + j) % experts), x)

    def hello_line(j):
        k = (mine + 1 + j) % line
        greet(line_at(k), k % dps)

    each(experts - 1, hello_experts)
    each(experts - 1, hello_sources)
    each(line - 1, hello_line)
    pl.semaphore_wait(pltpu.get_barrier_semaphore(), 2 * (experts - 1) + line - 1)

    for i in range(chunks):

        def row_out(j, i=i):
            d = (as_expert + 1 + j) % experts
            send(
                rows_ref.at[i, d],
                recv.at[i, as_source],
                row_send.at[i],
                row_recv.at[i],
                expert_at(d),
                x,
            )

        each(experts - 1, row_out)
        recv[i, as_source] = rows_ref[i, as_expert]

    tile_copy.wait()
    row_tiles, col_tiles = part // LANES, hidden // LANES
    for m, weight in enumerate((up, down)):
        for r in range(row_tiles):
            for k in range(col_tiles):
                s = (m * row_tiles + r) * col_tiles + k
                weight[r * LANES : (r + 1) * LANES, k * LANES : (k + 1) * LANES] = tiles[
                    map_ref[0, s]
                ]

    def to_hidden(i):
        wait_bytes(recv.at[i, pl.ds(0, experts - 1)], row_recv.at[i])
        rows = recv[i].reshape(experts * slots, part)
        product = jnp.dot(rows, up[...], preferred_element_type=jnp.float32)
        pre[i] = product.astype(jnp.bfloat16).reshape(dps, experts * slots // dps, hidden)

        def out(j):
            other = (x + 1 + j) % dps
            send(pre.at[i, other], sums.at[i, x], sum_send.at[i], sum_recv.at[i], me, other)

        each(dps - 1, out)

    def activate(i):
        wait_bytes(sums.at[i, pl.ds(0, dps - 1)], sum_recv.at[i])
        total = pre[i, x].astype(jnp.float32)
        for j in range(1, dps):
            total = total + sums[i, (x + j) % dps].astype(jnp.float32)
        hid[i, x] = (total * jax.nn.sigmoid(total)).astype(jnp.bfloat16)

        def out(j):
            send(
                hid.at[i, x], hid.at[i, x], hid_send.at[i], hid_recv.at[i], me, (x + 1 + j) % dps
            )

        each(dps - 1, out)

    def to_result(i):
        wait_bytes(hid.at[i, pl.ds(0, dps - 1)], hid_recv.at[i])
        units = hid[i].reshape(experts * slots, hidden)
        product = lax.dot_general(
            units, down[...], (((1,), (1,)), ((), ())), preferred_element_type=jnp.float32
        )
        res[i] = product.astype(jnp.bfloat16).reshape(experts, slots, part)

        def out(j):
            s = (as_source + 1 + j) % experts
            other = s // side
            slot = (z + other * (y - z)) * 2 + c
            send(res.at[i, s], ret.at[i, slot], ret_send.at[i], ret_recv.at[i], source_at(s), x)

        each(experts - 1, out)
        ret[i, as_expert] = res[i, as_source]

    def combine(i):
        wait_bytes(ret.at[i, pl.ds(0, experts - 1)], ret_recv.at[i])
        outs = ret[i].reshape(experts * slots, part)
        mixed = jnp.dot(comb_ref[i], outs, preferred_element_type=jnp.float32)
        mix[pl.ds(i * blocks, blocks)] = mixed.astype(jnp.bfloat16).reshape(blocks, tok, part)

        def out(j):
            k = i * blocks + (j + x) % blocks

            @pl.when(k != mine)
            def _():
                send(mix.at[k], fin.at[mine], fin_send, fin_recv, line_at(k), k % dps)

        each(blocks, out)

    steps = (to_hidden, activate, to_result, combine)
    lag = (0, 1, 2, 4)
    for turn in range(chunks + lag[-1]):
        for step, late in zip(steps, lag):
            if 0 <= turn - late < chunks:
                step(turn - late)

    fin[mine] = mix[mine]
    wait_bytes(fin.at[pl.ds(0, line - 1)], fin_recv)
    squares = jnp.zeros((tok, 1), jnp.float32)
    for g in range(dps):
        total = fin[g].astype(jnp.float32)
        for other in range(1, side):
            total = total + fin[other * dps + g].astype(jnp.float32)
        columns = slice(g * part, (g + 1) * part)
        layer = (tokens_ref[:, columns].astype(jnp.float32) + total).astype(jnp.bfloat16)
        out_ref[:, columns] = layer
        stream = layer.astype(jnp.float32)
        squares = squares + jnp.sum(stream * stream, axis=1, keepdims=True)
    renorm = lax.rsqrt(squares / (dps * part) + 1e-06)
    logits = jnp.zeros((tok, scores_ref.shape[1]), jnp.float32)
    for g in range(dps):
        stream = out_ref[:, g * part : (g + 1) * part].astype(jnp.float32)
        normed = (stream * renorm).astype(jnp.bfloat16)
        logits = logits + jnp.dot(normed, routers_ref[g], preferred_element_type=jnp.float32)
    scores_ref[...] = jax.nn.sigmoid(logits)

    wait_bytes(fin.at[pl.ds(0, line - 1)], fin_send)
    for i in range(chunks):
        wait_bytes(recv.at[i, pl.ds(0, experts - 1)], row_send.at[i])
        wait_bytes(sums.at[i, pl.ds(0, dps - 1)], sum_send.at[i])
        wait_bytes(hid.at[i, pl.ds(0, dps - 1)], hid_send.at[i])
        wait_bytes(ret.at[i, pl.ds(0, experts - 1)], ret_send.at[i])


def vmem():
    return pl.BlockSpec(memory_space=pltpu.VMEM)


def per_device(side, tokens, norm_gain, router, next_router, expert_ids, store, send_list, cache_map):
    tok, width = tokens.shape
    dps = lax.axis_size("dp")
    experts = router.shape[1]
    top = expert_ids.shape[1]
    tiles = cache_map.shape[1]
    part = width // dps
    row_tiles = part // LANES
    hidden = tiles // (2 * row_tiles) * LANES
    line = side * dps
    chunks = 4 if side % 4 == 0 else 1
    slots = line // chunks * CAP
    bf16 = jnp.bfloat16

    owned = store.reshape(tiles, LANES, LANES)
    leaving = owned[jnp.maximum(send_list.reshape(-1), 0)]
    arrived = lax.all_to_all(leaving, "ep", split_axis=0, concat_axis=0, tiled=True)

    values = tokens.astype(jnp.float32)
    scale = lax.rsqrt(jnp.mean(values * values, axis=1, keepdims=True) + 1e-06)
    normed = (values * scale * norm_gain).astype(bf16)
    scores = jax.nn.sigmoid(jnp.dot(normed, router, preferred_element_type=jnp.float32))
    chosen = (expert_ids[:, :, None] == jnp.arange(experts, dtype=jnp.int32)).astype(jnp.float32)
    picked = jnp.sum(chosen * scores[:, None, :], axis=2)
    weights = (2.5 * picked / jnp.sum(picked, axis=1, keepdims=True)).astype(bf16)
    named = jnp.sum(chosen, axis=1)
    earlier = jnp.cumsum(named, axis=0) - named
    rank = jnp.sum(earlier[:, None, :] * chosen, axis=2).astype(jnp.int32)
    core = lax.axis_index("ep") % 2
    y, z, c = expert_ids // (2 * side), (expert_ids // 2) % side, expert_ids % 2
    turned = jnp.where(core == 1, z * (2 * side) + y * 2 + c, expert_ids)
    match = (turned * CAP + rank)[:, :, None] == jnp.arange(experts * CAP, dtype=jnp.int32)
    combine = jnp.sum(jnp.where(match, weights.astype(jnp.float32)[:, :, None], 0.0), axis=1)
    combine = combine.astype(bf16).reshape(tok, side, experts * CAP // side).transpose(1, 0, 2)
    combine = jnp.pad(combine, ((0, 0), (0, 0), (0, LANES - combine.shape[2])))
    pay = jnp.concatenate(
        [
            jnp.broadcast_to(
                normed.reshape(tok, dps, part).transpose(1, 0, 2)[:, None], (dps, side, tok, part)
            ),
            jnp.broadcast_to(combine[None], (dps, side, tok, LANES)),
        ],
        axis=3,
    )
    depth = line // chunks * tok
    rows, comb, routers = pl.pallas_call(
        functools.partial(gather_kernel, side, dps, chunks, part),
        out_shape=(
            jax.ShapeDtypeStruct((chunks, 2 * side, slots, part), bf16),
            jax.ShapeDtypeStruct((chunks, depth, 2 * side * slots), bf16),
            jax.ShapeDtypeStruct((dps, part, next_router.shape[1]), bf16),
        ),
        in_specs=[vmem()] * 2,
        out_specs=(vmem(),) * 3,
        scratch_shapes=[pltpu.VMEM((line, tok, part + LANES), bf16)]
        + [pltpu.SemaphoreType.DMA] * 4,
        compiler_params=pltpu.CompilerParams(
            collective_id=0, has_side_effects=True, vmem_limit_bytes=24 << 20
        ),
    )(pay, next_router)

    rows_all = 2 * side * slots
    shared = pltpu.VMEM((chunks, dps, rows_all // dps, hidden), bf16)
    traded = pltpu.VMEM((chunks, 2 * side, slots, part), bf16)
    lined = pltpu.VMEM((line, tok, part), bf16)
    dma = pltpu.SemaphoreType.DMA((chunks,))
    return pl.pallas_call(
        functools.partial(layer_kernel, side, dps, chunks),
        out_shape=(
            jax.ShapeDtypeStruct((tok, width), bf16),
            jax.ShapeDtypeStruct((tok, next_router.shape[1]), jnp.float32),
        ),
        in_specs=[
            vmem(),
            vmem(),
            pl.BlockSpec(memory_space=pl.ANY),
            pl.BlockSpec(memory_space=pltpu.SMEM),
            vmem(),
            vmem(),
        ],
        out_specs=(vmem(), vmem()),
        scratch_shapes=[
            pltpu.VMEM(arrived.shape, bf16),
            pltpu.VMEM((part, hidden), bf16),
            pltpu.VMEM((part, hidden), bf16),
            traded,
            shared,
            shared,
            shared,
            traded,
            traded,
            lined,
            lined,
            pltpu.SemaphoreType.DMA,
        ]
        + [dma] * 8
        + [pltpu.SemaphoreType.DMA] * 2,
        compiler_params=pltpu.CompilerParams(
            collective_id=1, has_side_effects=True, vmem_limit_bytes=56 << 20
        ),
    )(rows, comb, arrived, cache_map, tokens, routers)


def solution(mesh):
    side = round((mesh.shape["ep"] // 2) ** 0.5)
    in_specs = (
        P(("ep", "dp"), None),
        P(),
        P(),
        P("dp", None),
        P(("ep", "dp"), None),
        P("ep", "dp", None, None, None),
        P("ep", None),
        P("ep", None),
    )
    out_specs = (P(("ep", "dp"), None), P(("ep", "dp"), None))
    return jax.shard_map(
        functools.partial(per_device, side),
        mesh=mesh,
        in_specs=in_specs,
        out_specs=out_specs,
        check_vma=False,
    )
```

time: 359 us -> 238 us (0.66)
  the two profiles are of different devices: /device:TPU:8 before, /device:TPU:48 now
where the time goes in v1:
time: 238 us
  Pallas kernels  206 us (87%)
  starting transfers between devices  17.9 us (8%)
  local copies, waits for them, and re-layouts  11.2 us (5%)
    pallas_call x1, Pallas kernels, per_device(): pl.pallas_call(functools.partial(gather_kernel, side, dps, chunks, part),...  105 us
    pallas_call x1, Pallas kernels, per_device(): pl.pallas_call(functools.partial(layer_kernel, side, dps, chunks), out_sh...  101 us
    all_to_all x1, starting transfers between devices, per_device(): lax.all_to_all(leaving, 'ep', split_axis=0, concat_axis=0, tiled=True)  17.9 us
    unnamed x20, local copies, waits for them, and re-layouts  5.91 us
    gather x1, local copies, waits for them, and re-layouts, per_device(): leaving = owned[jnp.maximum(send_list.reshape(-1), 0)]  5.09 us
  transfers between devices with their start and end apart: 1, of which 0 were waited for; matrix products, arithmetic and copies ran while one was open for 1% of the time, Pallas kernels for 44%

profile of v1, /device:TPU:48, one launch (start us, length us, event | category | flops | bytes accessed | tf_op | source)
XLA Modules:
  0.0 238.0 jit_solution(191299702512789140)
XLA Ops:
  0.6 0.0 copy-start
  0.6 0.7 maximum_bitcast_fusion
  1.4 5.1 %gather_fusion = bf16[128,128,128]{2,1,0:T(8,128)(2,1)} fusion(bf16[112,128,128]{2,1,0:T(8,128)(2,1)} %bitcast.13, s32[1024]{0:T(1024)S(1)} %pad_clamp_fusion), kind=kCustom, calls=%fused_computation | custom fusion | bytes 8389120 | tf_op jit(solution)/shard_map/gather | solution.py:357
  6.5 0.0 copy-start.7
  6.5 0.0 copy-start.5
  6.5 0.0 copy-start.6
  6.5 17.9 %all-to-all-start = ((bf16[128,128,128]{2,1,0:T(8,128)(2,1)}), bf16[128,128,128]{2,1,0:T(8,128)(2,1)}, u32[]{:S(2)}, u32[]{:S(2)}) async-start(bf16[128,128,128]{2,1,0:T(8,128)(2,1)} %gather_fusion), calls=%async_computation | async-start | bytes 8388608 | tf_op jit(solution)/shard_map/all_to_all | solution.py:358
  24.4 0.0 copy-start.4
  24.4 0.0 copy-done.7
  24.5 0.1 copy.18
  24.5 0.1 convert_reduce_fusion
  24.7 0.0 copy-done.5
  24.7 0.1 fusion.3
  24.8 0.0 copy-done.6
  24.8 0.1 fusion.5
  24.9 0.0 copy-done
  24.9 0.2 fusion.2
  25.2 0.3 select_reduce_fusion.1
  25.5 0.1 fusion.17
  25.6 0.1 select_reduce_fusion
  25.8 0.1 convert_element_type.42
  25.9 0.1 broadcast_in_dim.12
  26.0 0.2 pad_maximum_fusion.pay_ref
  26.2 0.0 copy-done.4
  26.2 105.3 %shard_map.95 = (bf16[4,16,16,896]{3,2,1,0:T(8,128)(2,1)S(1)}, bf16[4,128,256]{2,1,0:T(8,128)(2,1)S(1)}, bf16[4,896,128]{2,1,0:T(8,128)(2,1)S(1)}) custom-call(bf16[4,8,16,1024]{3,2,1,0:T(8,128)(2,1)S(1)} %pad_maximum_fusion.pay_ref, bf16[896,128]{1,0:T(8,128)(2,1)S(1)} %copy-done.4), custom_call_target="tpu_custom_call" | custom-call | tf_op jit(solution)/shard_map/pallas_call | solution.py:387
  131.5 0.0 copy-start.1
  131.5 1.3 copy-done.1
  132.8 0.0 copy-start.2
  132.8 1.0 copy-done.2
  133.8 0.0 copy-start.3
  133.8 0.7 copy-done.3
  134.5 0.0 all-to-all-done.tiles_hbm
  134.5 100.6 %shard_map.96 = (bf16[16,3584]{1,0:T(8,128)(2,1)}, f32[16,128]{1,0:T(8,128)}) custom-call(bf16[4,16,16,896]{3,2,1,0:T(8,128)(2,1)} %copy-done.1, bf16[4,128,256]{2,1,0:T(8,128)(2,1)} %copy-done.3, bf16[128,128,128]{2,1,0:T(8,128)(2,1)} %all-to-all-done.tiles_hbm, s32[1,112]{1,0:T(1,128)} %map_ref.1, bf16[16,3584]{1,0:T(8,128)(2,1)} %tokens_ref.1, ...), custom_call_target="tpu_custom_call" | custom-call | tf_op jit(solution)/shard_map/pallas_call | solution.py:408
  235.1 1.6 copy.31
  236.7 1.3 copy.32
  (9 shorter events, 0.1 us)
Async XLA Ops:
  0.6 24.3 %copy-start = (bf16[3584,128]{1,0:T(8,128)(2,1)S(1)}, bf16[3584,128]{1,0:T(8,128)(2,1)}, u32[]{:S(2)}) copy-start(bf16[3584,128]{1,0:T(8,128)(2,1)} %param.10) | copy-start | bytes 2752516
  6.5 18.0 %copy-start.7 = (s32[16,8]{0,1:T(8,128)S(1)}, s32[16,8]{0,1:T(8,128)}, u32[]{:S(2)}) copy-start(s32[16,8]{0,1:T(8,128)} %param.12) | copy-start | bytes 1540
  6.5 18.2 %copy-start.5 = (bf16[16,3584]{1,0:T(8,128)(2,1)S(1)}, bf16[16,3584]{1,0:T(8,128)(2,1)}, u32[]{:S(2)}) copy-start(bf16[16,3584]{1,0:T(8,128)(2,1)} %tokens_ref.1) | copy-start | bytes 344068
  6.5 18.3 %copy-start.6 = (f32[3584]{0:T(1024)S(1)}, f32[3584]{0:T(1024)}, u32[]{:S(2)}) copy-start(f32[3584]{0:T(1024)} %param.9) | copy-start | bytes 43012
  6.5 128.0 %all-to-all-start = ((bf16[128,128,128]{2,1,0:T(8,128)(2,1)}), bf16[128,128,128]{2,1,0:T(8,128)(2,1)}, u32[]{:S(2)}, u32[]{:S(2)}) async-start(bf16[128,128,128]{2,1,0:T(8,128)(2,1)} %gather_fusion), calls=%async_computation | async-start | bytes 8388608 | tf_op jit(solution)/shard_map/all_to_all | solution.py:358
  24.4 1.8 copy-start.4
  131.5 1.3 copy-start.1
  132.8 1.0 copy-start.2
  133.8 0.7 copy-start.3

commit v2 on v1

v2 whole, which is shorter than its diff:
```python
import functools

import jax
import jax.numpy as jnp
from jax import lax
from jax.experimental import pallas as pl
from jax.experimental.pallas import tpu as pltpu
from jax.sharding import PartitionSpec as P

MESH = pl.DeviceIdType.MESH
CAP = 2
LANES = 128
LAG = (0, 1, 2, 3, 4, 6)
ORDER = -1


def place(side):
    e = lax.axis_index("ep")
    x = lax.axis_index("dp")
    y, z, c = e // (2 * side), (e // 2) % side, e % 2
    a = y + c * (z - y)
    b = z + c * (y - z)
    return x, y, z, c, a, b


def on_line(side, a, b, c):
    wide, narrow = 2 * side - c * (2 * side - 2), 2 + c * (2 * side - 2)
    return a * wide + b * narrow


def send(src, dst, send_sem, recv_sem, ep, dp):
    pltpu.make_async_remote_copy(
        src_ref=src,
        dst_ref=dst,
        send_sem=send_sem,
        recv_sem=recv_sem,
        device_id={"ep": ep, "dp": dp},
        device_id_type=MESH,
    ).start()


def wait_bytes(ref, sem):
    pltpu.make_async_copy(ref, ref, sem).wait()


def greet(ep, dp):
    pl.semaphore_signal(
        pltpu.get_barrier_semaphore(), inc=1, device_id={"ep": ep, "dp": dp}, device_id_type=MESH
    )


def each(count, body):
    def step(j, carry):
        body(j)
        return carry

    lax.fori_loop(0, count, step, 0)


def layer_kernel(
    side,
    dps,
    chunks,
    pay_ref,
    router_ref,
    store_hbm,
    list_ref,
    map_ref,
    tokens_ref,
    out_ref,
    scores_ref,
    store,
    leave,
    mid,
    arrived,
    up,
    down,
    got,
    rows_out,
    comb_all,
    routers,
    recv,
    pre,
    half,
    sums,
    hid,
    res,
    ret,
    mix,
    fin,
    store_sem,
    got_send,
    got_recv,
    router_send,
    router_recv,
    leave_send,
    mid_recv,
    tile_send,
    tile_recv,
    row_send,
    row_recv,
    half_send,
    half_recv,
    sum_send,
    sum_recv,
    hid_send,
    hid_recv,
    pass_send,
    pass_recv,
    ret_send,
    ret_recv,
    fin_send,
    fin_recv,
):
    x, y, z, c, a, b = place(side)
    me = lax.axis_index("ep")
    line = side * dps
    mine = a * dps + x
    experts = 2 * side
    as_expert = b * 2 + c
    as_source = c * side + b
    part, hidden = up.shape
    slots = recv.shape[2]
    tok = tokens_ref.shape[0]
    blocks = line // chunks
    right, left, far = (x + 1) % dps, (x + dps - 1) % dps, (x + 2) % dps

    store_copy = pltpu.make_async_copy(store_hbm, store, store_sem)
    store_copy.start()

    def expert_at(d):
        return on_line(side, a, d // 2, c) + d % 2

    def source_at(s):
        other, i = s // side, s % side
        first = y * 2 * side + i * 2
        second = i * 2 * side + z * 2 + 1
        return first + other * (second - first)

    def line_at(k):
        return on_line(side, k // dps, b, c) + c

    def hello_experts(j):
        greet(expert_at((as_expert + 1 + j) % experts), x)

    def hello_sources(j):
        greet(source_at((as_source + 1 + j) % experts), x)

    def hello_line(j):
        k = (mine + 1 + j) % line
        greet(line_at(k), k % dps)

    each(experts - 1, hello_experts)
    each(experts - 1, hello_sources)
    each(line - 1, hello_line)
    pl.semaphore_wait(pltpu.get_barrier_semaphore(), 2 * (experts - 1) + line - 1)

    def token_out(j):
        k = (mine + 1 + j) % line
        send(pay_ref.at[k % dps, k // dps], got.at[mine], got_send, got_recv, line_at(k), k % dps)

    each(line - 1, token_out)

    steps_b = [(d, (side - d) % side) for d in range(side // 2 - 1, 0, -1)]
    steps_b.insert(1 if side > 2 else 0, (side // 2, 0))
    store_copy.wait()
    for i in range(chunks):

        def pick(j, i=i):
            there = (a + 1 + j) % side
            for q in range(4):
                ep = on_line(side, there, (b + steps_b[i][q // 2]) % side, c) + q % 2
                leave[i, j, q] = store[jnp.maximum(list_ref[0, ep], 0)]

        each(side, pick)

        def tile_out(j, i=i):
            there = (a + 1 + j) % side
            send(
                leave.at[i, j],
                mid.at[i, a],
                leave_send.at[i],
                mid_recv.at[i],
                on_line(side, there, b, c) + c,
                x,
            )

        each(side - 1, tile_out)
        mid[i, a] = leave[i, side - 1]

    def router_out(j):
        send(router_ref, routers.at[x], router_send, router_recv, me, (x + 1 + j) % dps)

    each(dps - 1, router_out)
    got[mine] = pay_ref[x, a]
    routers[x] = router_ref[...]

    depth = blocks * tok
    width = experts * slots
    q = lax.broadcasted_iota(jnp.int32, (width, LANES), 0)
    k = lax.broadcasted_iota(jnp.int32, (width, LANES), 1)
    pick_t = (k == (q // slots) * CAP + q % CAP).astype(jnp.float32).astype(jnp.bfloat16)
    q = lax.broadcasted_iota(jnp.int32, (LANES, width), 1)
    k = lax.broadcasted_iota(jnp.int32, (LANES, width), 0)
    pick_n = (k == (q // slots) * CAP + q % CAP).astype(jnp.float32).astype(jnp.bfloat16)
    r = lax.broadcasted_iota(jnp.int32, (depth, width), 0)
    q = lax.broadcasted_iota(jnp.int32, (depth, width), 1)
    own = r // tok == (q % slots) // CAP
    r = lax.broadcasted_iota(jnp.int32, (width, depth), 1)
    q = lax.broadcasted_iota(jnp.int32, (width, depth), 0)
    own_t = r // tok == (q % slots) // CAP
    wait_bytes(got.at[pl.ds(0, line - 1)], got_recv)
    for i in range(chunks):
        piece = got[i * blocks : (i + 1) * blocks].reshape(depth, part + LANES)
        comb = piece[:, part:]
        spread = jnp.dot(comb, pick_n, preferred_element_type=jnp.float32)
        comb_all[i] = jnp.where(own, spread, 0.0).astype(jnp.bfloat16)
        spread_t = lax.dot_general(
            pick_t, comb, (((1,), (1,)), ((), ())), preferred_element_type=jnp.float32
        )
        named = jnp.where(own_t & (spread_t != 0.0), 1.0, 0.0).astype(jnp.bfloat16)
        rows = jnp.dot(named, piece[:, :part], preferred_element_type=jnp.float32)
        rows_out[i] = rows.astype(jnp.bfloat16).reshape(experts, slots, part)

    def rows_away(i):
        def out(j):
            d = (as_expert + 1 + j) % experts
            send(
                rows_out.at[i, d],
                recv.at[i, as_source],
                row_send.at[i],
                row_recv.at[i],
                expert_at(d),
                x,
            )

        each(experts - 1, out)
        recv[i, as_source] = rows_out[i, as_expert]

    for i in range(chunks):
        wait_bytes(mid.at[i, pl.ds(0, side - 1)], mid_recv.at[i])
        if i == chunks - 1:
            rows_away(0)
        for q in range(4):
            ahead = steps_b[i][q // 2]
            ep = on_line(side, a, (b + ahead) % side, c) + q % 2

            def tile_on(i=i, q=q, ep=ep):
                send(mid.at[i, :, q], arrived.at[as_source], tile_send, tile_recv, ep, x)

            if ahead:
                tile_on()
            else:
                pl.when(c != q % 2)(tile_on)

                @pl.when(c == q % 2)
                def _(i=i, q=q):
                    arrived[as_source] = mid[i, :, q]

    for i in range(1, chunks):
        rows_away(i)

    wait_bytes(arrived.at[pl.ds(0, experts - 1)], tile_recv)
    row_tiles, col_tiles = part // LANES, hidden // LANES
    for m, weight in enumerate((up, down)):

        def assemble(r, m=m, weight=weight):
            for k in range(col_tiles):
                n = map_ref[0, (m * row_tiles + r) * col_tiles + k]
                yn, zn, cn = n // (2 * side), (n // 2) % side, n % 2
                along = cn * (zn - yn)
                tile = arrived[cn * side + zn - along, yn + along]
                weight[pl.ds(pl.multiple_of(r * LANES, LANES), LANES), pl.ds(k * LANES, LANES)] = (
                    tile
                )

        each(row_tiles, assemble)

    rows_each = experts * slots // dps
    cut = rows_each // 2

    def to_hidden(i):
        wait_bytes(recv.at[i, pl.ds(0, experts - 1)], row_recv.at[i])
        rows = recv[i].reshape(experts * slots, part)
        product = jnp.dot(rows, up[...], preferred_element_type=jnp.float32)
        pre[i] = product.astype(jnp.bfloat16).reshape(dps, rows_each, hidden)
        top, low = pl.ds(0, cut), pl.ds(cut, cut)
        send(pre.at[i, far, top], half.at[i, 0], half_send.at[i], half_recv.at[i], me, right)
        send(pre.at[i, far, low], half.at[i, 1], half_send.at[i], half_recv.at[i], me, left)

    def relay(i):
        wait_bytes(half.at[i], half_recv.at[i])
        for k, (other, start) in enumerate(((right, 0), (left, cut))):
            piece = pl.ds(start, cut)
            total = pre[i, other, piece].astype(jnp.float32) + half[i, k].astype(jnp.float32)
            pre[i, other, piece] = total.astype(jnp.bfloat16)
            send(pre.at[i, other], sums.at[i, k], sum_send.at[i], sum_recv.at[i], me, other)

    def activate(i):
        wait_bytes(sums.at[i], sum_recv.at[i])
        total = pre[i, x].astype(jnp.float32)
        total = total + sums[i, 0].astype(jnp.float32) + sums[i, 1].astype(jnp.float32)
        hid[i, x] = (total * jax.nn.sigmoid(total)).astype(jnp.bfloat16)
        for other in (right, left):
            send(hid.at[i, x], hid.at[i, x], hid_send.at[i], hid_recv.at[i], me, other)

    def pass_on(i):
        wait_bytes(sums.at[i], hid_recv.at[i])
        for other, source, start in ((right, left, 0), (left, right, cut)):
            piece = hid.at[i, source, pl.ds(start, cut)]
            send(piece, piece, pass_send.at[i], pass_recv.at[i], me, other)

    def to_result(i):
        wait_bytes(half.at[i], pass_recv.at[i])
        units = hid[i].reshape(experts * slots, hidden)
        product = lax.dot_general(
            units, down[...], (((1,), (1,)), ((), ())), preferred_element_type=jnp.float32
        )
        res[i] = product.astype(jnp.bfloat16).reshape(experts, slots, part)

        def out(j):
            s = (as_source + 1 + j) % experts
            other = s // side
            slot = (z + other * (y - z)) * 2 + c
            send(res.at[i, s], ret.at[i, slot], ret_send.at[i], ret_recv.at[i], source_at(s), x)

        each(experts - 1, out)
        ret[i, as_expert] = res[i, as_source]

    def combine(i):
        wait_bytes(ret.at[i, pl.ds(0, experts - 1)], ret_recv.at[i])
        outs = ret[i].reshape(experts * slots, part)
        mixed = jnp.dot(comb_all[i], outs, preferred_element_type=jnp.float32)
        mix[pl.ds(i * blocks, blocks)] = mixed.astype(jnp.bfloat16).reshape(blocks, tok, part)

        def out(j):
            k = i * blocks + (j + x) % blocks

            @pl.when(k != mine)
            def _():
                send(mix.at[k], fin.at[mine], fin_send, fin_recv, line_at(k), k % dps)

        each(blocks, out)

    steps = (to_hidden, relay, activate, pass_on, to_result, combine)
    for turn in range(chunks + LAG[-1]):
        for step, late in sorted(zip(steps, LAG), key=lambda p: ORDER * p[1]):
            if 0 <= turn - late < chunks:
                step(turn - late)

    fin[mine] = mix[mine]
    wait_bytes(routers.at[pl.ds(0, dps - 1)], router_recv)
    wait_bytes(fin.at[pl.ds(0, line - 1)], fin_recv)
    squares = jnp.zeros((tok, 1), jnp.float32)
    for g in range(dps):
        total = fin[g].astype(jnp.float32)
        for other in range(1, side):
            total = total + fin[other * dps + g].astype(jnp.float32)
        columns = slice(g * part, (g + 1) * part)
        layer = (tokens_ref[:, columns].astype(jnp.float32) + total).astype(jnp.bfloat16)
        out_ref[:, columns] = layer
        stream = layer.astype(jnp.float32)
        squares = squares + jnp.sum(stream * stream, axis=1, keepdims=True)
    renorm = lax.rsqrt(squares / (dps * part) + 1e-06)
    logits = jnp.zeros((tok, scores_ref.shape[1]), jnp.float32)
    for g in range(dps):
        stream = out_ref[:, g * part : (g + 1) * part].astype(jnp.float32)
        normed = (stream * renorm).astype(jnp.bfloat16)
        logits = logits + jnp.dot(normed, routers[g], preferred_element_type=jnp.float32)
    scores_ref[...] = jax.nn.sigmoid(logits)

    wait_bytes(got.at[pl.ds(0, line - 1)], got_send)
    wait_bytes(routers.at[pl.ds(0, dps - 1)], router_send)
    wait_bytes(arrived.at[pl.ds(0, experts - 1)], tile_send)
    wait_bytes(fin.at[pl.ds(0, line - 1)], fin_send)
    for i in range(chunks):
        wait_bytes(mid.at[i, pl.ds(0, side - 1)], leave_send.at[i])
        wait_bytes(recv.at[i, pl.ds(0, experts - 1)], row_send.at[i])
        wait_bytes(half.at[i], half_send.at[i])
        wait_bytes(sums.at[i], sum_send.at[i])
        wait_bytes(sums.at[i], hid_send.at[i])
        wait_bytes(half.at[i], pass_send.at[i])
        wait_bytes(ret.at[i, pl.ds(0, experts - 1)], ret_send.at[i])


def vmem():
    return pl.BlockSpec(memory_space=pltpu.VMEM)


def per_device(side, tokens, norm_gain, router, next_router, expert_ids, store, send_list, cache_map):
    tok, width = tokens.shape
    dps = lax.axis_size("dp")
    experts = router.shape[1]
    top = expert_ids.shape[1]
    tiles = cache_map.shape[1]
    part = width // dps
    row_tiles = part // LANES
    hidden = tiles // (2 * row_tiles) * LANES
    line = side * dps
    chunks = side // 2
    slots = line // chunks * CAP
    bf16 = jnp.bfloat16

    values = tokens.astype(jnp.float32)
    scale = lax.rsqrt(jnp.mean(values * values, axis=1, keepdims=True) + 1e-06)
    normed = (values * scale * norm_gain).astype(bf16)
    scores = jax.nn.sigmoid(jnp.dot(normed, router, preferred_element_type=jnp.float32))
    chosen = (expert_ids[:, :, None] == jnp.arange(experts, dtype=jnp.int32)).astype(jnp.float32)
    picked = jnp.sum(chosen * scores[:, None, :], axis=2)
    weights = (2.5 * picked / jnp.sum(picked, axis=1, keepdims=True)).astype(bf16)
    named = jnp.sum(chosen, axis=1)
    earlier = jnp.cumsum(named, axis=0) - named
    rank = jnp.sum(earlier[:, None, :] * chosen, axis=2).astype(jnp.int32)
    core = lax.axis_index("ep") % 2
    y, z, c = expert_ids // (2 * side), (expert_ids // 2) % side, expert_ids % 2
    turned = jnp.where(core == 1, z * (2 * side) + y * 2 + c, expert_ids)
    match = (turned * CAP + rank)[:, :, None] == jnp.arange(experts * CAP, dtype=jnp.int32)
    combine = jnp.sum(jnp.where(match, weights.astype(jnp.float32)[:, :, None], 0.0), axis=1)
    combine = combine.astype(bf16).reshape(tok, side, experts * CAP // side).transpose(1, 0, 2)
    combine = jnp.pad(combine, ((0, 0), (0, 0), (0, LANES - combine.shape[2])))
    pay = jnp.concatenate(
        [
            jnp.broadcast_to(
                normed.reshape(tok, dps, part).transpose(1, 0, 2)[:, None], (dps, side, tok, part)
            ),
            jnp.broadcast_to(combine[None], (dps, side, tok, LANES)),
        ],
        axis=3,
    )
    rows_all = 2 * side * slots
    shared = pltpu.VMEM((chunks, dps, rows_all // dps, hidden), bf16)
    paired = pltpu.VMEM((chunks, 2, rows_all // dps, hidden), bf16)
    halves = pltpu.VMEM((chunks, 2, rows_all // dps // 2, hidden), bf16)
    traded = pltpu.VMEM((chunks, 2 * side, slots, part), bf16)
    lined = pltpu.VMEM((line, tok, part), bf16)
    weight = pltpu.VMEM((part, hidden), bf16)
    moved = pltpu.VMEM((chunks, side, 4, LANES, LANES), bf16)
    one = pltpu.SemaphoreType.DMA
    many = pltpu.SemaphoreType.DMA((chunks,))
    return pl.pallas_call(
        functools.partial(layer_kernel, side, dps, chunks),
        out_shape=(
            jax.ShapeDtypeStruct((tok, width), bf16),
            jax.ShapeDtypeStruct((tok, next_router.shape[1]), jnp.float32),
        ),
        in_specs=[
            vmem(),
            vmem(),
            pl.BlockSpec(memory_space=pl.ANY),
            pl.BlockSpec(memory_space=pltpu.SMEM),
            pl.BlockSpec(memory_space=pltpu.SMEM),
            vmem(),
        ],
        out_specs=(vmem(), vmem()),
        scratch_shapes=[
            pltpu.VMEM((tiles, LANES, LANES), bf16),
            moved,
            moved,
            pltpu.VMEM((2 * side, side, LANES, LANES), bf16),
            weight,
            weight,
            pltpu.VMEM((line, tok, part + LANES), bf16),
            traded,
            pltpu.VMEM((chunks, line // chunks * tok, rows_all), bf16),
            pltpu.VMEM((dps, part, next_router.shape[1]), bf16),
            traded,
            shared,
            halves,
            paired,
            shared,
            traded,
            traded,
            lined,
            lined,
        ]
        + [one] * 5
        + [many] * 2
        + [one] * 2
        + [many] * 12
        + [one] * 2,
        compiler_params=pltpu.CompilerParams(
            collective_id=0, has_side_effects=True, vmem_limit_bytes=58 << 20
        ),
    )(pay, next_router, store.reshape(tiles, LANES, LANES), send_list, cache_map, tokens)


def solution(mesh):
    side = round((mesh.shape["ep"] // 2) ** 0.5)
    in_specs = (
        P(("ep", "dp"), None),
        P(),
        P(),
        P("dp", None),
        P(("ep", "dp"), None),
        P("ep", "dp", None, None, None),
        P("ep", None),
        P("ep", None),
    )
    out_specs = (P(("ep", "dp"), None), P(("ep", "dp"), None))
    return jax.shard_map(
        functools.partial(per_device, side),
        mesh=mesh,
        in_specs=in_specs,
        out_specs=out_specs,
        check_vma=False,
    )
```

time: 238 us -> 212 us (0.89)
  starting transfers between devices: 17.9 us -> 0 us
  local copies, waits for them, and re-layouts: 11.2 us -> 3.83 us
  Pallas kernels: 206 us -> 203 us
    pallas_call x1 -> x0, Pallas kernels: 105 us -> none  [per_device(): pl.pallas_call(functools.partial(gather_kernel, side, dps, chunks, part),...]
    pallas_call x1, Pallas kernels: 101 us -> 203 us  [per_device(): pl.pallas_call(functools.partial(layer_kernel, side, dps, chunks), out_sh...]
    all_to_all x1 -> x0, starting transfers between devices: 17.9 us -> none  [per_device(): lax.all_to_all(leaving, 'ep', split_axis=0, concat_axis=0, tiled=True)]
    gather x1 -> x0, local copies, waits for them, and re-layouts: 5.09 us -> none  [per_device(): leaving = owned[jnp.maximum(send_list.reshape(-1), 0)]]
    unnamed x20 -> x6, local copies, waits for them, and re-layouts: 5.91 us -> 3.63 us
  transfers between devices with their start and end apart: 1 -> 0, of which waited for: 0 -> 0; matrix products, arithmetic and copies ran while one was open for 1% -> 0% of each run, Pallas kernels for 44% -> 0%
where the time goes in v2:
time: 212 us
  Pallas kernels  203 us (96%)
  other arithmetic  3.96 us (2%)
  local copies, waits for them, and re-layouts  3.83 us (2%)
    pallas_call x1, Pallas kernels, per_device(): pl.pallas_call(functools.partial(layer_kernel, side, dps, chunks), out_sh...  203 us

profile of v2, /device:TPU:48, one launch (start us, length us, event | category | flops | bytes accessed | tf_op | source)
XLA Modules:
  0.0 212.0 jit_solution(12175974291153636849)
XLA Ops:
  0.6 0.0 copy-start
  0.7 1.1 fusion.3
  1.8 0.8 copy.18
  2.5 0.1 convert_reduce_fusion
  2.7 1.0 fusion.5
  3.7 0.0 copy-done
  3.7 0.2 fusion.2
  3.9 0.3 select_reduce_fusion.1
  4.3 0.1 fusion.17
  4.4 0.1 select_reduce_fusion
  4.5 0.1 convert_element_type.42
  4.7 0.1 broadcast_in_dim.12
  4.8 1.2 pad_maximum_fusion.pay_ref
  5.9 203.3 %shard_map.95 = (bf16[16,3584]{1,0:T(8,128)(2,1)}, f32[16,128]{1,0:T(8,128)}) custom-call(bf16[4,8,16,1024]{3,2,1,0:T(8,128)(2,1)} %pad_maximum_fusion.pay_ref, bf16[896,128]{1,0:T(8,128)(2,1)} %router_ref.1, bf16[112,128,128]{2,1,0:T(8,128)(2,1)} %bitcast.11, s32[1,128]{1,0:T(1,128)} %list_ref.1, s32[1,112]{1,0:T(1,128)} %map_ref.1, bf16[16,3584]{1,0:T(8,128)(2,1)} %tokens_ref.1), custom_call_target="tpu_custom_call" | custom-call | tf_op jit(solution)/shard_map/pallas_call | solution.py:440
  209.2 1.6 copy.31
  210.7 1.3 copy.32
  (8 shorter events, 0.1 us)
Async XLA Ops:
  0.6 3.1 %copy-start = (bf16[3584,128]{1,0:T(8,128)(2,1)S(1)}, bf16[3584,128]{1,0:T(8,128)(2,1)}, u32[]{:S(2)}) copy-start(bf16[3584,128]{1,0:T(8,128)(2,1)} %param.10) | copy-start | bytes 2752516

commit v3 on v2

--- a/solution.py
+++ b/solution.py
@@ -1,4 +1,5 @@
 import functools
+import types
 
 import jax
 import jax.numpy as jnp
@@ -10,7 +11,8 @@
 MESH = pl.DeviceIdType.MESH
 CAP = 2
 LANES = 128
-LAG = (0, 1, 2, 3, 4, 6)
+PIECES = 4
+LAG = (0, 1, 2, 3, 4, 9)
 ORDER = -1
 
 
@@ -57,61 +59,38 @@
     lax.fori_loop(0, count, step, 0)
 
 
+def hops_along(side):
+    pairs = [(d, (side - d) % side) for d in range(side // 2 - 1, 0, -1)]
+    pairs.insert(1 if side > 2 else 0, (side // 2, 0))
+    return pairs
+
+
 def layer_kernel(
     side,
     dps,
     chunks,
-    pay_ref,
+    names,
+    tokens_ref,
+    gain_ref,
     router_ref,
-    store_hbm,
+    next_ref,
+    ids_ref,
     list_ref,
     map_ref,
-    tokens_ref,
+    store_hbm,
     out_ref,
     scores_ref,
-    store,
-    leave,
-    mid,
-    arrived,
-    up,
-    down,
-    got,
-    rows_out,
-    comb_all,
-    routers,
-    recv,
-    pre,
-    half,
-    sums,
-    hid,
-    res,
-    ret,
-    mix,
-    fin,
-    store_sem,
-    got_send,
-    got_recv,
-    router_send,
-    router_recv,
-    leave_send,
-    mid_recv,
-    tile_send,
-    tile_recv,
-    row_send,
-    row_recv,
-    half_send,
-    half_recv,
-    sum_send,
-    sum_recv,
-    hid_send,
-    hid_recv,
-    pass_send,
-    pass_recv,
-    ret_send,
-    ret_recv,
-    fin_send,
-    fin_recv,
+    *scratch,
 ):
+    own_refs = types.SimpleNamespace(**dict(zip(names, scratch)))
+    pay = own_refs.pay
+    (store, mid, arrived, up, down, got, rows_out, comb_all, routers, recv) = scratch[:10]
+    (pre, half, sums, hid, res, ret, mix, fin) = scratch[10:18]
+    (store_sem, gx_send, gx_recv, router_send, router_recv, tile_send, tile_recv) = scratch[18:25]
+    (fin_send, fin_recv, row_send, row_recv, half_send, half_recv) = scratch[25:31]
+    (sum_send, sum_recv, hid_send, hid_recv, pass_send, pass_recv) = scratch[31:37]
+    (ret_send, ret_recv, ag_send, ag_recv, along_send, along_recv) = scratch[37:43]
+    (over_send, over_recv) = scratch[43:45]
     x, y, z, c, a, b = place(side)
     me = lax.axis_index("ep")
     line = side * dps
@@ -123,6 +102,8 @@
     slots = recv.shape[2]
     tok = tokens_ref.shape[0]
     blocks = line // chunks
+    last = side // 2
+    ways = ((0, 1), (1, side - 1))
     right, left, far = (x + 1) % dps, (x + dps - 1) % dps, (x + 2) % dps
 
     store_copy = pltpu.make_async_copy(store_hbm, store, store_sem)
@@ -155,72 +136,173 @@
     each(line - 1, hello_line)
     pl.semaphore_wait(pltpu.get_barrier_semaphore(), 2 * (experts - 1) + line - 1)
 
-    def token_out(j):
-        k = (mine + 1 + j) % line
-        send(pay_ref.at[k % dps, k // dps], got.at[mine], got_send, got_recv, line_at(k), k % dps)
-
-    each(line - 1, token_out)
-
-    steps_b = [(d, (side - d) % side) for d in range(side // 2 - 1, 0, -1)]
-    steps_b.insert(1 if side > 2 else 0, (side // 2, 0))
-    store_copy.wait()
-    for i in range(chunks):
-
-        def pick(j, i=i):
-            there = (a + 1 + j) % side
-            for q in range(4):
-                ep = on_line(side, there, (b + steps_b[i][q // 2]) % side, c) + q % 2
-                leave[i, j, q] = store[jnp.maximum(list_ref[0, ep], 0)]
-
-        each(side, pick)
-
-        def tile_out(j, i=i):
-            there = (a + 1 + j) % side
-            send(
-                leave.at[i, j],
-                mid.at[i, a],
-                leave_send.at[i],
-                mid_recv.at[i],
-                on_line(side, there, b, c) + c,
-                x,
+    def route():
+        values = tokens_ref[...].astype(jnp.float32)
+        scale = lax.rsqrt(jnp.mean(values * values, axis=1, keepdims=True) + 1e-06)
+        normed = (values * scale * gain_ref[...]).astype(jnp.bfloat16)
+        logits = jnp.dot(normed, router_ref[...], preferred_element_type=jnp.float32)
+        scores = jax.nn.sigmoid(logits)
+        count = scores.shape[1]
+        top = ids_ref.shape[0]
+        ids = lax.dot_general(
+            (
+                lax.broadcasted_iota(jnp.int32, (tok, tok), 0)
+                == lax.broadcasted_iota(jnp.int32, (tok, tok), 1)
+            ).astype(jnp.float32),
+            ids_ref[...].astype(jnp.float32),
+            (((1,), (1,)), ((), ())),
+            preferred_element_type=jnp.float32,
+        ).astype(jnp.int32)
+        lane = lax.broadcasted_iota(jnp.int32, (tok, count), 1)
+        hits = [(ids[:, k : k + 1] == lane).astype(jnp.float32) for k in range(top)]
+        picked = [jnp.sum(hit * scores, axis=1, keepdims=True) for hit in hits]
+        total = functools.reduce(jnp.add, picked)
+        weights = [(2.5 * p / total).astype(jnp.bfloat16).astype(jnp.float32) for p in picked]
+        weight = functools.reduce(jnp.add, [hit * w for hit, w in zip(hits, weights)])
+        named = functools.reduce(jnp.add, hits)
+        earlier = (
+            lax.broadcasted_iota(jnp.int32, (tok, tok), 0)
+            > lax.broadcasted_iota(jnp.int32, (tok, tok), 1)
+        ).astype(jnp.float32)
+        rank = jnp.dot(earlier, named, preferred_element_type=jnp.float32)
+        lanes = pay.shape[2] - part
+        e = lax.broadcasted_iota(jnp.int32, (count, lanes), 0)
+        column = lax.broadcasted_iota(jnp.int32, (count, lanes), 1)
+        ye, ze, ce = e // (2 * side), (e // 2) % side, e % 2
+        turn_y, turn_z = ye + c * (ze - ye), ze + c * (ye - ze)
+        first = (turn_y * (2 * side) + turn_z * 2 + ce) * CAP
+        combine = jnp.zeros((tok, lanes), jnp.float32)
+        for r in range(CAP):
+            ranked = jnp.where(rank == r, weight, 0.0).astype(jnp.bfloat16)
+            place_r = (column == first + r).astype(jnp.float32).astype(jnp.bfloat16)
+            combine = combine + jnp.dot(ranked, place_r, preferred_element_type=jnp.float32)
+        for g in range(dps):
+            pay[g, :, :part] = normed[:, g * part : (g + 1) * part]
+            pay[g, :, part:] = combine.astype(jnp.bfloat16)
+
+    def tokens_out():
+        def out(j):
+            other = (x + 1 + j) % dps
+            send(pay.at[other], got.at[a, x], gx_send, gx_recv, me, other)
+
+        each(dps - 1, out)
+        got[a, x] = pay[x]
+
+    def tokens_step(k):
+        if k == 0:
+            wait_bytes(got.at[a, pl.ds(0, dps - 1)], gx_recv)
+        else:
+            for d, step in ways:
+                block = got.at[0] if k < last else got.at[0, pl.ds(0, dps // 2)]
+                wait_bytes(block, ag_recv.at[d, k - 1])
+        if k == last:
+            return
+        for d, step in ways:
+            origin = (a + side - k if d == 0 else a + k) % side
+            block = got.at[origin]
+            if k + 1 == last:
+                block = got.at[origin, pl.ds(d * (dps // 2), dps // 2)]
+            to = on_line(side, (a + step) % side, b, c) + c
+            send(block, block, ag_send.at[d, k], ag_recv.at[d, k], to, x)
+
+    pairs = hops_along(side)
+    outs, ins = own_refs.out1, [None] + [getattr(own_refs, f"in{k}") for k in range(1, last + 1)]
+
+    def tile_for(i, q, h, there):
+        ep = on_line(side, there, (b + pairs[i][q]) % side, c) + h
+        return store[jnp.maximum(list_ref[0, ep], 0)]
+
+    def along_start(i):
+        for d, step in ways:
+
+            def near(j, d=d):
+                there = (a + 1 + j if d == 0 else a + side - 1 - j) % side
+                for h in range(2):
+                    for q in range(2):
+                        outs[d, i, 2 * j + h, q] = tile_for(i, q, h, there)
+
+            if last > 1:
+                each(last - 1, near)
+            for q in range(2):
+                outs[d, i, 2 * (last - 1), q] = tile_for(i, q, d, (a + last) % side)
+            to = on_line(side, (a + step) % side, b, c) + c
+            send(outs.at[d, i], ins[1].at[d, i], along_send.at[d, i, 0], along_recv.at[d, i, 0], to, x)
+        for h in range(2):
+            for q in range(2):
+                mid[i, q, h, a] = tile_for(i, q, h, a)
+
+    def along_step(i, k):
+        for d, step in ways:
+            wait_bytes(ins[k].at[d, i], along_recv.at[d, i, k - 1])
+            if k < last:
+                rest = ins[k].at[d, i, pl.ds(2, side - 1 - 2 * k)]
+                to = on_line(side, (a + step) % side, b, c) + c
+                send(
+                    rest, ins[k + 1].at[d, i], along_send.at[d, i, k], along_recv.at[d, i, k], to, x
+                )
+        for d, step in ways:
+            origin = (a + side - k if d == 0 else a + k) % side
+            for h in (0, 1) if k < last else (d,):
+                for q in range(2):
+                    mid[i, q, h, origin] = ins[k][d, i, h if k < last else 0, q]
+
+    def over_hops(i):
+        return min(pairs[i][0], side - pairs[i][0])
+
+    def over_step(i, k):
+        hops = over_hops(i)
+        split = hops == last
+        trail = getattr(own_refs, f"over{i}")
+        for d, step in ways:
+            if k == 1:
+                block = mid.at[i, 0, d] if split else mid.at[i, d]
+            else:
+                block = trail.at[k - 2, d]
+                wait_bytes(block, over_recv.at[d, i, k - 2])
+            to = on_line(side, a, (b + step) % side, c)
+            origin = c * side + (b + side - k + 1 if d == 0 else b + k - 1) % side
+            if k < hops:
+                sems = over_send.at[d, i, k - 1], over_recv.at[d, i, k - 1]
+                send(block, trail.at[k - 1, d], *sems, to + c, x)
+            elif split:
+                send(block, arrived.at[origin], tile_send, tile_recv, to + d, x)
+            else:
+                for h in range(2):
+                    send(block.at[h], arrived.at[origin], tile_send, tile_recv, to + h, x)
+        if split and k == 1:
+            pair = me + 1 - 2 * c
+            send(mid.at[i, 1, 1 - c], arrived.at[as_source], tile_send, tile_recv, pair, x)
+            arrived[as_source] = mid[i, 1, c]
+
+    def build_rows():
+        depth = blocks * tok
+        width = experts * slots
+        lanes = got.shape[3] - part
+        first = a * experts * CAP
+        q = lax.broadcasted_iota(jnp.int32, (width, lanes), 0)
+        k = lax.broadcasted_iota(jnp.int32, (width, lanes), 1)
+        pick_t = (k == first + (q // slots) * CAP + q % CAP).astype(jnp.float32).astype(jnp.bfloat16)
+        q = lax.broadcasted_iota(jnp.int32, (lanes, width), 1)
+        k = lax.broadcasted_iota(jnp.int32, (lanes, width), 0)
+        pick_n = (k == first + (q // slots) * CAP + q % CAP).astype(jnp.float32).astype(jnp.bfloat16)
+        r = lax.broadcasted_iota(jnp.int32, (depth, width), 0)
+        q = lax.broadcasted_iota(jnp.int32, (depth, width), 1)
+        own = r // tok == (q % slots) // CAP
+        r = lax.broadcasted_iota(jnp.int32, (width, depth), 1)
+        q = lax.broadcasted_iota(jnp.int32, (width, depth), 0)
+        own_t = r // tok == (q % slots) // CAP
+        lines = got.shape[0] // chunks
+        for i in range(chunks):
+            piece = got[i * lines : (i + 1) * lines].reshape(depth, part + lanes)
+            comb = piece[:, part:]
+            spread = jnp.dot(comb, pick_n, preferred_element_type=jnp.float32)
+            comb_all[i] = jnp.where(own, spread, 0.0).astype(jnp.bfloat16)
+            spread_t = lax.dot_general(
+                pick_t, comb, (((1,), (1,)), ((), ())), preferred_element_type=jnp.float32
             )
-
-        each(side - 1, tile_out)
-        mid[i, a] = leave[i, side - 1]
-
-    def router_out(j):
-        send(router_ref, routers.at[x], router_send, router_recv, me, (x + 1 + j) % dps)
-
-    each(dps - 1, router_out)
-    got[mine] = pay_ref[x, a]
-    routers[x] = router_ref[...]
-
-    depth = blocks * tok
-    width = experts * slots
-    q = lax.broadcasted_iota(jnp.int32, (width, LANES), 0)
-    k = lax.broadcasted_iota(jnp.int32, (width, LANES), 1)
-    pick_t = (k == (q // slots) * CAP + q % CAP).astype(jnp.float32).astype(jnp.bfloat16)
-    q = lax.broadcasted_iota(jnp.int32, (LANES, width), 1)
-    k = lax.broadcasted_iota(jnp.int32, (LANES, width), 0)
-    pick_n = (k == (q // slots) * CAP + q % CAP).astype(jnp.float32).astype(jnp.bfloat16)
-    r = lax.broadcasted_iota(jnp.int32, (depth, width), 0)
-    q = lax.broadcasted_iota(jnp.int32, (depth, width), 1)
-    own = r // tok == (q % slots) // CAP
-    r = lax.broadcasted_iota(jnp.int32, (width, depth), 1)
-    q = lax.broadcasted_iota(jnp.int32, (width, depth), 0)
-    own_t = r // tok == (q % slots) // CAP
-    wait_bytes(got.at[pl.ds(0, line - 1)], got_recv)
-    for i in range(chunks):
-        piece = got[i * blocks : (i + 1) * blocks].reshape(depth, part + LANES)
-        comb = piece[:, part:]
-        spread = jnp.dot(comb, pick_n, preferred_element_type=jnp.float32)
-        comb_all[i] = jnp.where(own, spread, 0.0).astype(jnp.bfloat16)
-        spread_t = lax.dot_general(
-            pick_t, comb, (((1,), (1,)), ((), ())), preferred_element_type=jnp.float32
-        )
-        named = jnp.where(own_t & (spread_t != 0.0), 1.0, 0.0).astype(jnp.bfloat16)
-        rows = jnp.dot(named, piece[:, :part], preferred_element_type=jnp.float32)
-        rows_out[i] = rows.astype(jnp.bfloat16).reshape(experts, slots, part)
+            named = jnp.where(own_t & (spread_t != 0.0), 1.0, 0.0).astype(jnp.bfloat16)
+            rows = jnp.dot(named, piece[:, :part], preferred_element_type=jnp.float32)
+            rows_out[i] = rows.astype(jnp.bfloat16).reshape(experts, slots, part)
 
     def rows_away(i):
         def out(j):
@@ -237,25 +319,33 @@
         each(experts - 1, out)
         recv[i, as_source] = rows_out[i, as_expert]
 
-    for i in range(chunks):
-        wait_bytes(mid.at[i, pl.ds(0, side - 1)], mid_recv.at[i])
-        if i == chunks - 1:
-            rows_away(0)
-        for q in range(4):
-            ahead = steps_b[i][q // 2]
-            ep = on_line(side, a, (b + ahead) % side, c) + q % 2
-
-            def tile_on(i=i, q=q, ep=ep):
-                send(mid.at[i, :, q], arrived.at[as_source], tile_send, tile_recv, ep, x)
-
-            if ahead:
-                tile_on()
-            else:
-                pl.when(c != q % 2)(tile_on)
-
-                @pl.when(c == q % 2)
-                def _(i=i, q=q):
-                    arrived[as_source] = mid[i, :, q]
+    def router_out(j):
+        send(next_ref, routers.at[x], router_send, router_recv, me, (x + 1 + j) % dps)
+
+    store_copy.wait()
+    loads = len(pairs)
+    late = min(1, loads - 1)
+    for turn in range(loads + 2 * last):
+        if turn < loads:
+            along_start(turn)
+        if turn == 0:
+            route()
+            tokens_out()
+            each(dps - 1, router_out)
+            routers[x] = next_ref[...]
+        if late <= turn <= last + late:
+            tokens_step(turn - late)
+        for k in range(1, last + 1):
+            if 0 <= turn - k < loads:
+                along_step(turn - k, k)
+        if turn == last + late:
+            build_rows()
+        for k in range(1, last + 1):
+            i = turn - last - k + 1
+            if 0 <= i < loads and k <= over_hops(i):
+                if k == 1 and i == loads - 1:
+                    rows_away(0)
+                over_step(i, k)
 
     for i in range(1, chunks):
         rows_away(i)
@@ -369,12 +459,20 @@
         logits = logits + jnp.dot(normed, routers[g], preferred_element_type=jnp.float32)
     scores_ref[...] = jax.nn.sigmoid(logits)
 
-    wait_bytes(got.at[pl.ds(0, line - 1)], got_send)
+    wait_bytes(got.at[0, pl.ds(0, dps - 1)], gx_send)
+    for d, step in ways:
+        for k in range(last):
+            block = got.at[0] if k + 1 < last else got.at[0, pl.ds(0, dps // 2)]
+            wait_bytes(block, ag_send.at[d, k])
+            for i in range(loads):
+                wait_bytes(ins[k + 1].at[d, i], along_send.at[d, i, k])
+        for i in range(loads):
+            for k in range(1, over_hops(i)):
+                wait_bytes(getattr(own_refs, f"over{i}").at[0, d], over_send.at[d, i, k - 1])
     wait_bytes(routers.at[pl.ds(0, dps - 1)], router_send)
     wait_bytes(arrived.at[pl.ds(0, experts - 1)], tile_send)
     wait_bytes(fin.at[pl.ds(0, line - 1)], fin_send)
     for i in range(chunks):
-        wait_bytes(mid.at[i, pl.ds(0, side - 1)], leave_send.at[i])
         wait_bytes(recv.at[i, pl.ds(0, experts - 1)], row_send.at[i])
         wait_bytes(half.at[i], half_send.at[i])
         wait_bytes(sums.at[i], sum_send.at[i])
@@ -397,36 +495,11 @@
     row_tiles = part // LANES
     hidden = tiles // (2 * row_tiles) * LANES
     line = side * dps
-    chunks = side // 2
+    chunks = min(PIECES, side)
     slots = line // chunks * CAP
     bf16 = jnp.bfloat16
 
-    values = tokens.astype(jnp.float32)
-    scale = lax.rsqrt(jnp.mean(values * values, axis=1, keepdims=True) + 1e-06)
-    normed = (values * scale * norm_gain).astype(bf16)
-    scores = jax.nn.sigmoid(jnp.dot(normed, router, preferred_element_type=jnp.float32))
-    chosen = (expert_ids[:, :, None] == jnp.arange(experts, dtype=jnp.int32)).astype(jnp.float32)
-    picked = jnp.sum(chosen * scores[:, None, :], axis=2)
-    weights = (2.5 * picked / jnp.sum(picked, axis=1, keepdims=True)).astype(bf16)
-    named = jnp.sum(chosen, axis=1)
-    earlier = jnp.cumsum(named, axis=0) - named
-    rank = jnp.sum(earlier[:, None, :] * chosen, axis=2).astype(jnp.int32)
-    core = lax.axis_index("ep") % 2
-    y, z, c = expert_ids // (2 * side), (expert_ids // 2) % side, expert_ids % 2
-    turned = jnp.where(core == 1, z * (2 * side) + y * 2 + c, expert_ids)
-    match = (turned * CAP + rank)[:, :, None] == jnp.arange(experts * CAP, dtype=jnp.int32)
-    combine = jnp.sum(jnp.where(match, weights.astype(jnp.float32)[:, :, None], 0.0), axis=1)
-    combine = combine.astype(bf16).reshape(tok, side, experts * CAP // side).transpose(1, 0, 2)
-    combine = jnp.pad(combine, ((0, 0), (0, 0), (0, LANES - combine.shape[2])))
-    pay = jnp.concatenate(
-        [
-            jnp.broadcast_to(
-                normed.reshape(tok, dps, part).transpose(1, 0, 2)[:, None], (dps, side, tok, part)
-            ),
-            jnp.broadcast_to(combine[None], (dps, side, tok, LANES)),
-        ],
-        axis=3,
-    )
+    lanes = experts * CAP + -(experts * CAP) % LANES
     rows_all = 2 * side * slots
     shared = pltpu.VMEM((chunks, dps, rows_all // dps, hidden), bf16)
     paired = pltpu.VMEM((chunks, 2, rows_all // dps, hidden), bf16)
@@ -434,54 +507,70 @@
     traded = pltpu.VMEM((chunks, 2 * side, slots, part), bf16)
     lined = pltpu.VMEM((line, tok, part), bf16)
     weight = pltpu.VMEM((part, hidden), bf16)
-    moved = pltpu.VMEM((chunks, side, 4, LANES, LANES), bf16)
-    one = pltpu.SemaphoreType.DMA
-    many = pltpu.SemaphoreType.DMA((chunks,))
+    pairs = hops_along(side)
+    last = side // 2
+    tile = (LANES, LANES)
+
+    def sems(*shape):
+        return pltpu.SemaphoreType.DMA(shape)
+
+    scratch = [
+        ("store", pltpu.VMEM((tiles, *tile), bf16)),
+        ("mid", pltpu.VMEM((len(pairs), 2, 2, side, *tile), bf16)),
+        ("arrived", pltpu.VMEM((2 * side, side, *tile), bf16)),
+        ("up", weight),
+        ("down", weight),
+        ("got", pltpu.VMEM((side, dps, tok, part + lanes), bf16)),
+        ("rows_out", traded),
+        ("comb_all", pltpu.VMEM((chunks, line // chunks * tok, rows_all), bf16)),
+        ("routers", pltpu.VMEM((dps, part, next_router.shape[1]), bf16)),
+        ("recv", traded),
+        ("pre", shared),
+        ("half", halves),
+        ("sums", paired),
+        ("hid", shared),
+        ("res", traded),
+        ("ret", traded),
+        ("mix", lined),
+        ("fin", lined),
+    ]
+    scratch += [(f"one{k}", pltpu.SemaphoreType.DMA) for k in range(9)]
+    scratch += [(f"many{k}", sems(chunks)) for k in range(12)]
+    scratch += [(f"ring{k}", sems(2, last)) for k in range(2)]
+    scratch += [(f"path{k}", sems(2, len(pairs), last)) for k in range(4)]
+    scratch += [("out1", pltpu.VMEM((2, len(pairs), side - 1, 2, *tile), bf16))]
+    scratch += [("pay", pltpu.VMEM((dps, tok, part + lanes), bf16))]
+    for k in range(1, last + 1):
+        scratch += [(f"in{k}", pltpu.VMEM((2, len(pairs), side + 1 - 2 * k, 2, *tile), bf16))]
+    for i, (one_way, _) in enumerate(pairs):
+        inner = (side,) if one_way == last else (2, side)
+        scratch += [(f"over{i}", pltpu.VMEM((max(1, one_way - 1), 2, *inner, *tile), bf16))]
     return pl.pallas_call(
-        functools.partial(layer_kernel, side, dps, chunks),
+        functools.partial(
+            layer_kernel, side, dps, chunks, tuple(name for name, _ in scratch)
+        ),
         out_shape=(
             jax.ShapeDtypeStruct((tok, width), bf16),
             jax.ShapeDtypeStruct((tok, next_router.shape[1]), jnp.float32),
         ),
-        in_specs=[
-            vmem(),
-            vmem(),
-            pl.BlockSpec(memory_space=pl.ANY),
-            pl.BlockSpec(memory_space=pltpu.SMEM),
-            pl.BlockSpec(memory_space=pltpu.SMEM),
-            vmem(),
-        ],
+        in_specs=[vmem()] * 5
+        + [pl.BlockSpec(memory_space=pltpu.SMEM)] * 2
+        + [pl.BlockSpec(memory_space=pl.ANY)],
         out_specs=(vmem(), vmem()),
-        scratch_shapes=[
-            pltpu.VMEM((tiles, LANES, LANES), bf16),
-            moved,
-            moved,
-            pltpu.VMEM((2 * side, side, LANES, LANES), bf16),
-            weight,
-            weight,
-            pltpu.VMEM((line, tok, part + LANES), bf16),
-            traded,
-            pltpu.VMEM((chunks, line // chunks * tok, rows_all), bf16),
-            pltpu.VMEM((dps, part, next_router.shape[1]), bf16),
-            traded,
-            shared,
-            halves,
-            paired,
-            shared,
-            traded,
-            traded,
-            lined,
-            lined,
-        ]
-        + [one] * 5
-        + [many] * 2
-        + [one] * 2
-        + [many] * 12
-        + [one] * 2,
+        scratch_shapes=[shape for _, shape in scratch],
         compiler_params=pltpu.CompilerParams(
-            collective_id=0, has_side_effects=True, vmem_limit_bytes=58 << 20
+            collective_id=0, has_side_effects=True, vmem_limit_bytes=60 << 20
         ),
-    )(pay, next_router, store.reshape(tiles, LANES, LANES), send_list, cache_map, tokens)
+    )(
+        tokens,
+        norm_gain[None],
+        router,
+        next_router,
+        expert_ids.T,
+        send_list,
+        cache_map,
+        store.reshape(tiles, LANES, LANES),
+    )
 
 
 def solution(mesh):

time: 212 us -> 201 us (0.948)
  the two profiles are of different devices: /device:TPU:48 before, /device:TPU:176 now
where the time goes in v3:
time: 201 us
  Pallas kernels  196 us (98%)
  local copies, waits for them, and re-layouts  4.17 us (2%)
    pallas_call x1, Pallas kernels, per_device(): pl.pallas_call(functools.partial(layer_kernel, side, dps, chunks, tuple((...  196 us

profile of v3, /device:TPU:176, one launch (start us, length us, event | category | flops | bytes accessed | tf_op | source)
XLA Modules:
  0.0 200.6 jit_solution(4663459567918031168)
XLA Ops:
  0.6 1.3 broadcast_in_dim.3.gain_ref
  2.0 195.8 %shard_map.95 = (bf16[16,3584]{1,0:T(8,128)(2,1)}, f32[16,128]{1,0:T(8,128)}) custom-call(bf16[16,3584]{1,0:T(8,128)(2,1)} %tokens_ref.1, f32[1,3584]{1,0:T(1,128)} %broadcast_in_dim.3.gain_ref, bf16[3584,128]{1,0:T(8,128)(2,1)} %router_ref.1, bf16[896,128]{1,0:T(8,128)(2,1)} %next_ref.1, s32[8,16]{1,0:T(8,128)} %bitcast.3, s32[1,128]{1,0:T(1,128)} %list_ref.1, ...), custom_call_target="tpu_custom_call" | custom-call | tf_op jit(solution)/shard_map/pallas_call | solution.py:548
  197.7 1.6 copy.12
  199.3 1.3 copy.13

commit v4 on v3

--- a/solution.py
+++ b/solution.py
@@ -61,7 +61,7 @@
 
 def hops_along(side):
     pairs = [(d, (side - d) % side) for d in range(side // 2 - 1, 0, -1)]
-    pairs.insert(1 if side > 2 else 0, (side // 2, 0))
+    pairs.insert(0, (side // 2, 0))
     return pairs
 
 
@@ -134,7 +134,6 @@
     each(experts - 1, hello_experts)
     each(experts - 1, hello_sources)
     each(line - 1, hello_line)
-    pl.semaphore_wait(pltpu.get_barrier_semaphore(), 2 * (experts - 1) + line - 1)
 
     def route():
         values = tokens_ref[...].astype(jnp.float32)
@@ -212,7 +211,7 @@
         ep = on_line(side, there, (b + pairs[i][q]) % side, c) + h
         return store[jnp.maximum(list_ref[0, ep], 0)]
 
-    def along_start(i):
+    def along_fill(i):
         for d, step in ways:
 
             def near(j, d=d):
@@ -225,11 +224,14 @@
                 each(last - 1, near)
             for q in range(2):
                 outs[d, i, 2 * (last - 1), q] = tile_for(i, q, d, (a + last) % side)
-            to = on_line(side, (a + step) % side, b, c) + c
-            send(outs.at[d, i], ins[1].at[d, i], along_send.at[d, i, 0], along_recv.at[d, i, 0], to, x)
         for h in range(2):
             for q in range(2):
                 mid[i, q, h, a] = tile_for(i, q, h, a)
+
+    def along_start(i):
+        for d, step in ways:
+            to = on_line(side, (a + step) % side, b, c) + c
+            send(outs.at[d, i], ins[1].at[d, i], along_send.at[d, i, 0], along_recv.at[d, i, 0], to, x)
 
     def along_step(i, k):
         for d, step in ways:
@@ -322,14 +324,18 @@
     def router_out(j):
         send(next_ref, routers.at[x], router_send, router_recv, me, (x + 1 + j) % dps)
 
+    route()
     store_copy.wait()
+    along_fill(0)
+    pl.semaphore_wait(pltpu.get_barrier_semaphore(), 2 * (experts - 1) + line - 1)
     loads = len(pairs)
     late = min(1, loads - 1)
     for turn in range(loads + 2 * last):
         if turn < loads:
             along_start(turn)
+        if turn + 1 < loads:
+            along_fill(turn + 1)
         if turn == 0:
-            route()
             tokens_out()
             each(dps - 1, router_out)
             routers[x] = next_ref[...]
@@ -352,9 +358,9 @@
 
     wait_bytes(arrived.at[pl.ds(0, experts - 1)], tile_recv)
     row_tiles, col_tiles = part // LANES, hidden // LANES
-    for m, weight in enumerate((up, down)):
-
-        def assemble(r, m=m, weight=weight):
+
+    def assemble(m, weight):
+        def one_row(r):
             for k in range(col_tiles):
                 n = map_ref[0, (m * row_tiles + r) * col_tiles + k]
                 yn, zn, cn = n // (2 * side), (n // 2) % side, n % 2
@@ -364,8 +370,9 @@
                     tile
                 )
 
-        each(row_tiles, assemble)
-
+        each(row_tiles, one_row)
+
+    assemble(0, up)
     rows_each = experts * slots // dps
     cut = rows_each // 2
 
@@ -437,6 +444,8 @@
         for step, late in sorted(zip(steps, LAG), key=lambda p: ORDER * p[1]):
             if 0 <= turn - late < chunks:
                 step(turn - late)
+        if turn == 0:
+            assemble(1, down)
 
     fin[mine] = mix[mine]
     wait_bytes(routers.at[pl.ds(0, dps - 1)], router_recv)

time: 201 us -> 197 us (0.980)
  the two profiles are of different devices: /device:TPU:176 before, /device:TPU:112 now
where the time goes in v4:
time: 197 us
  Pallas kernels  192 us (97%)
  local copies, waits for them, and re-layouts  4.17 us (2%)
    pallas_call x1, Pallas kernels, per_device(): pl.pallas_call(functools.partial(layer_kernel, side, dps, chunks, tuple((...  192 us

profile of v4, /device:TPU:112, one launch (start us, length us, event | category | flops | bytes accessed | tf_op | source)
XLA Modules:
  0.0 196.6 jit_solution(3560661796440889742)
XLA Ops:
  0.6 1.3 broadcast_in_dim.3.gain_ref
  2.0 191.8 %shard_map.95 = (bf16[16,3584]{1,0:T(8,128)(2,1)}, f32[16,128]{1,0:T(8,128)}) custom-call(bf16[16,3584]{1,0:T(8,128)(2,1)} %tokens_ref.1, f32[1,3584]{1,0:T(1,128)} %broadcast_in_dim.3.gain_ref, bf16[3584,128]{1,0:T(8,128)(2,1)} %router_ref.1, bf16[896,128]{1,0:T(8,128)(2,1)} %next_ref.1, s32[8,16]{1,0:T(8,128)} %bitcast.3, s32[1,128]{1,0:T(1,128)} %list_ref.1, ...), custom_call_target="tpu_custom_call" | custom-call | tf_op jit(solution)/shard_map/pallas_call | solution.py:557
  193.7 1.6 copy.12
  195.3 1.3 copy.13
